TPU v7x, 256 devices: a whole 4x4x8 slice. The times are simulated.
256 devices in a mesh: dp: 8 (over z_hi, core), row: 8 (over y, z_lo), col: 4 (over x).
Axes of the slice: x: 4, y: 4, z: 8 (z_hi: 4, z_lo: 2; z = z_hi * 2 + z_lo), core: 2. Of those that a mesh axis runs over, the one named last changes fastest.
Arguments:
- activations: bfloat16 [8192, 4096], P('dp', 'col'), may hold values from -6 to 6
- out_grad: bfloat16 [8192, 14336], P('dp', 'row'), may hold values from -6 to 6
- weight: float32 [8, 1792, 4096], P('row', 'dp', 'col'), as said below
- step_size: float32 [8, 1792], P('row'), may hold values from 0.001 to 0.016
Outputs:
- input_grad: bfloat16 [8192, 4096], P(('dp', 'row'), 'col')
- weight_grad: float32 [8, 1792, 4096], P('row', 'dp', 'col')
- step_grad: float32 [8, 1792], P('row', 'dp')
Inputs may be any that keep to these rules, and one draw needn't show every extreme that they name: Each latent weight divided by its row's step lies at least 0.1 away from every multiple of one half.
All inputs are finite; a program needn't handle non-finite values.
Results may differ from a plain program's by a relative error of at most 0.0096.
Values may be sent and summed in bfloat16 or wider, within the bound.
A program may use at most 128 MiB of HBM per device.

v0:
```python
import jax
import jax.numpy as jnp
from jax import lax
from jax.sharding import Mesh
from jax.sharding import PartitionSpec as P

D = 4096
DP = ("dp_0", "dp_1")
DP_ROW = ("dp_0", "dp_1", "row")


def in_order(pieces, dim):
    shape = list(pieces.shape[1:])
    shape[dim] *= pieces.shape[0]
    return jnp.moveaxis(pieces, 0, dim).reshape(shape)


def gather_in_order(shard, axes, sequence):
    pieces = shard[None]
    for k in sequence:
        pieces = lax.all_gather(pieces, axes[k], axis=0, tiled=True)
    carried = [lax.axis_size(axes[k]) for k in reversed(sequence)]
    pieces = pieces.reshape(*carried, *shard.shape)
    turned = sorted(range(len(sequence)), key=lambda place: sequence[len(sequence) - 1 - place])
    return pieces.transpose(*turned, *range(len(sequence), pieces.ndim)).reshape(-1, *shard.shape)


def gathered_by_axis(shard, axes, sequence, dim):
    return in_order(gather_in_order(shard, axes, sequence), dim)


def cut_along(shard, dim, size):
    before, after = (shard.shape[:dim], shard.shape[dim + 1 :])
    return jnp.moveaxis(shard.reshape(*before, size, -1, *after), dim, 0)


def sum_at_owner(shard, axis, dim):
    pieces = cut_along(shard, dim, lax.axis_size(axis))
    arrived = lax.all_to_all(pieces, axis, split_axis=0, concat_axis=0, tiled=True)
    return arrived.astype(jnp.float32).sum(axis=0)


def quantize(latent, scales):
    ratio = latent / scales[:, None]
    clipped = jnp.clip(ratio, -8.0, 7.0)
    levels = jnp.floor(clipped + 0.5)
    inside = jnp.where((ratio >= -8.0) & (ratio <= 7.0), 1.0, 0.0).astype(jnp.float32)
    factor = jnp.where(inside > 0.5, levels - ratio, clipped)
    quantized = (levels * scales[:, None]).astype(jnp.bfloat16)
    return (quantized, inside, factor)


def shards(activations, out_grad, weight, step_size):
    own_count = weight.shape[1]
    position = lax.axis_index(DP)
    scales = step_size[0]
    own_scales = lax.dynamic_slice_in_dim(scales, position * own_count, own_count, 0)
    grad_factor = 1.0 / (7.0 * D) ** 0.5
    products = lax.dot_general(
        out_grad, activations, (((0,), (0,)), ((), ())), preferred_element_type=jnp.float32
    )
    own_quantized, own_inside, own_factor = quantize(weight[0], own_scales)
    quantized = gathered_by_axis(own_quantized, DP, (0, 1), 0)
    summed = lax.psum_scatter(
        products.astype(jnp.bfloat16), DP, scatter_dimension=0, tiled=True
    ).astype(jnp.float32)
    step_rows = lax.psum(jnp.sum(summed * own_factor, axis=1) * grad_factor, "col")
    weight_grad = (summed * own_inside)[None]
    input_grad = sum_at_owner(
        jnp.dot(out_grad, quantized, preferred_element_type=jnp.float32).astype(jnp.bfloat16),
        "row",
        0,
    ).astype(jnp.bfloat16)
    return (input_grad, weight_grad, step_rows[None])


def solution(mesh):
    split = Mesh(
        mesh.devices.reshape(4, 2, mesh.shape["row"], mesh.shape["col"]),
        ("dp_0", "dp_1", "row", "col"),
    )
    in_specs = (P(DP, "col"), P(DP, "row"), P("row", DP, "col"), P("row", None))
    out_specs = (P(DP_ROW, "col"), P("row", DP, "col"), P("row", DP))
    return jax.shard_map(
        shards, mesh=split, in_specs=in_specs, out_specs=out_specs, check_vma=False
    )
```

profile of v0, /device:TPU:8, one launch (start us, length us, event | category | flops | bytes accessed | tf_op | source)
XLA Modules:
  0.0 161.9 jit_solution(16024086718184774631)
XLA Ops:
  8.0 0.0 copy-start
  8.0 0.0 all-gather.3.cloned.1.call-start
  8.1 0.9 constant_dynamic-slice_fusion
  9.0 2.2 %multiply_convert_fusion = bf16[1,224,1024]{2,1,0:T(8,128)(2,1)} fusion(f32[1,224,1024]{2,1,0:T(8,128)} %param.6, f32[224]{0:T(256)S(1)} %bitcast.24), kind=kLoop, calls=%fused_computation.8 | loop fusion | flops 1376256 | bytes 1377152 | tf_op jit(solution)/shard_map/convert_element_type | solution.py:49
  11.2 0.0 all-gather.3.cloned.1.call-update
  11.2 0.0 all-gather.5.cloned.1.call-start
  11.2 48.6 %all-gather.3.cloned.1.call-done = bf16[4,224,1024]{2,1,0:T(8,128)(2,1)} async-done(((bf16[1,224,1024]{2,1,0:T(8,128)(2,1)}), bf16[4,224,1024]{2,1,0:T(8,128)(2,1)}) %all-gather.3.cloned.1.call-update) | async-done | bytes 1835024 | tf_op jit(solution)/shard_map/all_gather | solution.py:21
  59.9 0.0 all-gather.5.cloned.1.call-update
  59.9 0.0 reduce-scatter.2.cloned.1.call-start
  60.0 0.0 copy-done
  60.0 7.6 %convolution_convert_fusion = bf16[1792,1024]{1,0:T(8,128)(2,1)} fusion(bf16[1024,1792]{1,0:T(8,128)(2,1)} %param.5, bf16[1024,1024]{1,0:T(8,128)(2,1)S(1)} %copy-done), kind=kOutput, calls=%fused_computation | convolution fusion | flops 3759931392 | bytes 9437184 | tf_op jit(solution)/shard_map/dot_general | solution.py:59
  67.6 0.0 reduce-scatter.2.cloned.1.call-update
  67.6 12.4 %all-gather.5.cloned.1.call-done = bf16[8,224,1024]{2,1,0:T(8,128)(2,1)} async-done(((bf16[4,224,1024]{2,1,0:T(8,128)(2,1)}), bf16[8,224,1024]{2,1,0:T(8,128)(2,1)}) %all-gather.5.cloned.1.call-update) | async-done | bytes 3670032 | tf_op jit(solution)/shard_map/all_gather | solution.py:21
  80.0 0.0 copy-start.2
  80.0 2.6 %copy.8 = bf16[4,2,224,1024]{3,2,1,0:T(8,128)(2,1)S(1)} copy(bf16[4,2,224,1024]{3,2,0,1:T(8,128)(2,1)} %bitcast.21) | data formatting | bytes 7340032 | tf_op jit(solution)/shard_map/transpose | solution.py:25
  82.6 0.5 copy-done.2
  83.1 5.2 %convolution_convert_fusion.1 = bf16[1024,1024]{0,1:T(8,128)(2,1)} fusion(bf16[1024,1792]{1,0:T(8,128)(2,1)S(1)} %copy-done.2, bf16[1792,1024]{1,0:T(8,128)(2,1)S(1)} %bitcast.22), kind=kOutput, calls=%fused_computation.1 | convolution fusion | flops 3759144960 | bytes 9437184 | tf_op jit(solution)/shard_map/dot_general | solution.py:70
  88.3 0.0 copy-start.1
  88.3 5.9 %all-to-all-start = ((bf16[8,128,1024]{2,1,0:T(8,128)(2,1)}), bf16[8,128,1024]{2,1,0:T(8,128)(2,1)}, u32[]{:S(2)}, u32[]{:S(2)}) async-start(bf16[8,128,1024]{2,1,0:T(8,128)(2,1)} %bitcast.23), calls=%async_computation | async-start | bytes 4194304 | tf_op jit(solution)/shard_map/all_to_all | solution.py:39
  94.2 44.0 %reduce-scatter.2.cloned.1.call-done = bf16[224,1024]{1,0:T(8,128)(2,1)} async-done(((bf16[1792,1024]{1,0:T(8,128)(2,1)}), bf16[224,1024]{1,0:T(8,128)(2,1)}) %reduce-scatter.2.cloned.1.call-update) | async-done | bytes 458768 | tf_op jit(solution)/shard_map/reduce_scatter | solution.py:64
  138.3 0.0 copy-done.1
  138.3 2.5 %fusion = (f32[224]{0:T(256)S(1)}, f32[1,224,1024]{2,1,0:T(8,128)}) fusion(bf16[224,1024]{1,0:T(8,128)(2,1)} %reduce-scatter.2.cloned.1.call-done, f32[224]{0:T(256)S(1)} %bitcast.25, f32[1,224,1024]{2,1,0:T(8,128)S(1)} %copy-done.1), kind=kLoop, calls=%fused_computation.5 | loop fusion | flops 3440416 | bytes 2295552 | tf_op jit(solution)/shard_map/reduce_sum | solution.py:67
  140.8 10.9 %psum.7 = f32[1,224]{1,0:T(1,128)} all-reduce(f32[1,224]{1,0:T(1,128)S(1)} %bitcast.26), channel_id=1, replica_groups=mesh['dp_0'=4,'dp_1'=2,'row'=8,'col'=4] {'col'}, use_global_device_ids=true, to_apply=%region_3.4 | all-reduce | flops 224 | bytes 1792 | tf_op jit(solution)/shard_map/psum | solution.py:67
  151.7 0.0 all-to-all-done
  151.7 2.7 %reduce_sum.21 = bf16[128,1024]{1,0:T(8,128)(2,1)} reduce(bf16[8,128,1024]{2,1,0:T(8,128)(2,1)} %all-to-all-done, bf16[]{:T(256)} %constant.33.clone.1), dimensions={0}, to_apply=%region_0.1 | reduce | flops 917504 | bytes 2359298 | tf_op jit(solution)/shard_map/reduce_sum | solution.py:40
  (1 shorter events, 0.0 us)
Async XLA Ops:
  8.0 52.0 %copy-start = (bf16[1024,1024]{1,0:T(8,128)(2,1)S(1)}, bf16[1024,1024]{1,0:T(8,128)(2,1)}, u32[]{:S(2)}) copy-start(bf16[1024,1024]{1,0:T(8,128)(2,1)} %param.4) | copy-start | bytes 6291460
  8.0 51.9 %all-gather.3.cloned.1.call-start = ((), (), s32[]{:S(2)}) async-start(), calls=%async_computation.2 | async-start | bytes 2293760 | tf_op jit(solution)/shard_map/all_gather | solution.py:21
  11.2 68.8 %all-gather.5.cloned.1.call-start = ((), (), s32[]{:S(2)}) async-start(), calls=%async_computation.3 | async-start | bytes 5505024 | tf_op jit(solution)/shard_map/all_gather | solution.py:21
  59.9 78.4 %reduce-scatter.2.cloned.1.call-start = ((), (), s32[]{:S(2)}) async-start(), calls=%async_computation.4 | async-start | bytes 4128768 | tf_op jit(solution)/shard_map/reduce_scatter | solution.py:64
  80.0 3.1 %copy-start.2 = (bf16[1024,1792]{1,0:T(8,128)(2,1)S(1)}, bf16[1024,1792]{1,0:T(8,128)(2,1)}, u32[]{:S(2)}) copy-start(bf16[1024,1792]{1,0:T(8,128)(2,1)} %param.5) | copy-start | bytes 11010052
  88.3 50.0 %copy-start.1 = (f32[1,224,1024]{2,1,0:T(8,128)S(1)}, f32[1,224,1024]{2,1,0:T(8,128)}, u32[]{:S(2)}) copy-start(f32[1,224,1024]{2,1,0:T(8,128)} %param.6) | copy-start | bytes 2752516
  88.3 63.4 %all-to-all-start = ((bf16[8,128,1024]{2,1,0:T(8,128)(2,1)}), bf16[8,128,1024]{2,1,0:T(8,128)(2,1)}, u32[]{:S(2)}, u32[]{:S(2)}) async-start(bf16[8,128,1024]{2,1,0:T(8,128)(2,1)} %bitcast.23), calls=%async_computation | async-start | bytes 4194304 | tf_op jit(solution)/shard_map/all_to_all | solution.py:39
Sparse Core Ops, SparseCore 0:
  11.3 48.5 all-gather.2
  61.7 18.2 all-gather.4
Sparse Core Ops, SparseCore 1:
  67.7 70.5 reduce-scatter.1
where the time goes:
time: 162 us
  waiting for transfers between devices  105 us (65%)
  between operations  15.5 us (10%)
  matrix products  12.8 us (8%)
  blocking collectives  10.9 us (7%)
  other arithmetic  7.39 us (5%)
  starting transfers between devices  6.07 us (4%)
  local copies, waits for them, and re-layouts  4.04 us (2%)
    all_gather x2, waiting for transfers between devices, gather_in_order(): pieces = lax.all_gather(pieces, axes[k], axis=0, tiled=True)  61 us
    reduce_scatter x1, waiting for transfers between devices, shards(): lax.psum_scatter(products.astype(jnp.bfloat16), DP, scatter_dimension=0,...  44 us
    psum x1, blocking collectives, shards(): lax.psum(jnp.sum(summed * own_factor, axis=1) * grad_factor, 'col')  10.9 us
    dot_general x1, matrix products, shards(): lax.dot_general(out_grad, activations, (((0,), (0,)), ((), ())), preferre...  7.62 us
    all_to_all x1, starting transfers between devices, sum_at_owner(): lax.all_to_all(pieces, axis, split_axis=0, concat_axis=0, tiled=True)  5.94 us
    dot_general x1, matrix products, shards(): jnp.dot(out_grad, quantized, preferred_element_type=jnp.float32)  5.18 us
  transfers between devices with their start and end apart: 4, of which 3 were waited for; matrix products, arithmetic and copies ran while one was open for 11% of the time, Pallas kernels for 0%

commit v1 on v0

v1 whole, which is shorter than its diff:
```python
import functools

import jax
import jax.numpy as jnp
from jax import lax
from jax.experimental import pallas as pl
from jax.experimental.pallas import tpu as pltpu
from jax.sharding import Mesh
from jax.sharding import PartitionSpec as P

MESH = pl.DeviceIdType.MESH
D = 4096
DP = ("zh", "core")
ROW = ("y", "zl")
OWN = 224
HALF = 112
COLS = 1024
ROWS = 1792
TOKENS = 1024
SUB = 128
GRAD_FACTOR = 1.0 / (7.0 * D) ** 0.5

AG_RA, AG_RB, AG_LB, AG_LA, AG_FR, AG_FL = range(6)
D_OWN, D_LEFT, D_RIGHT, D_FAR = range(6, 10)
D_P = 10
RS_FR, RS_FL, RS_OR, RS_OL, RS_SR, RS_SL = range(14, 20)
Y_FU, Y_FD, Y_OU, Y_OD, Y_SU, Y_SD = range(20, 26)
Z_PAIR = 26
X_SUM = 27
N_COPIES = 30


def rows_of(index, size):
    return pl.ds(pl.multiple_of(index * size, size), size)


def kernel(
    act_hbm, og_hbm, w_hbm, s_hbm,
    ig_out, wg_out, sg_out,
    act, og, w, s, scol, ogt, q, fac, ins,
    p_own, p_snd, p_rcv, c_buf,
    rs_far, rs_own, rs_sum, rs_snd,
    g, gown, y_far, y_own, y_sum, y_snd, tot, z_snd, z_rcv,
    x_snd, x_rcv,
    ss, rs, ls,
):
    zh = lax.axis_index("zh")
    core = lax.axis_index("core")
    y = lax.axis_index("y")
    zl = lax.axis_index("zl")
    x = lax.axis_index("x")
    zr, zlft, zf = (zh + 1) % 4, (zh + 3) % 4, (zh + 2) % 4
    right, left = {"zh": zr}, {"zh": zlft}
    other = 1 - core
    peer = {"core": other}
    yu, yd, yf = (y + 1) % 4, (y + 3) % 4, (y + 2) % 4
    up, down = {"y": yu}, {"y": yd}
    pair = {"zl": 1 - zl}
    crosses = [{"x": (x + k) % 4} for k in (1, 2, 3)]

    loads = [
        pltpu.make_async_copy(w_hbm, w, ls.at[0]),
        pltpu.make_async_copy(s_hbm, s, ls.at[1]),
        pltpu.make_async_copy(og_hbm, og, ls.at[2]),
        pltpu.make_async_copy(act_hbm, act, ls.at[3]),
    ]
    for load in loads:
        load.start()

    barrier = pltpu.get_barrier_semaphore()
    partners = [right, left, peer, up, down, pair] + crosses
    for partner in partners:
        pl.semaphore_signal(barrier, inc=1, device_id=partner, device_id_type=MESH)

    def copy(src, dst, number, device):
        return pltpu.make_async_remote_copy(
            src_ref=src, dst_ref=dst, send_sem=ss.at[number], recv_sem=rs.at[number],
            device_id=device, device_id_type=MESH,
        )

    def shard(j, c):
        return q.at[rows_of(j * 2 + c, OWN)]

    def half(j, c, h):
        return q.at[rows_of((j * 2 + c) * 2 + h, HALF)]

    loads[1].wait()
    scol[...] = jnp.transpose(jnp.broadcast_to(s[...], (128, ROWS)))
    loads[0].wait()
    own_row = (zh * 2 + core) * OWN
    own_at = pl.ds(pl.multiple_of(own_row, OWN), OWN)
    scale = scol[own_at, :]
    for k in range(COLS // 128):
        at = slice(k * 128, (k + 1) * 128)
        ratio = w[:, at] / scale
        levels = jnp.floor(jnp.clip(ratio, -8.0, 7.0) + 0.5)
        q[own_at, at] = (levels * scale).astype(jnp.bfloat16)

    pl.semaphore_wait(barrier, len(partners))

    ag = {
        AG_RA: copy(half(zh, core, 0), half(zh, core, 0), AG_RA, right),
        AG_RB: copy(half(zh, core, 1), half(zh, core, 1), AG_RB, right),
        AG_LB: copy(half(zh, core, 1), half(zh, core, 1), AG_LB, left),
        AG_LA: copy(half(zh, core, 0), half(zh, core, 0), AG_LA, left),
        AG_FR: copy(half(zlft, core, 0), half(zlft, core, 0), AG_FR, right),
        AG_FL: copy(half(zr, core, 1), half(zr, core, 1), AG_FL, left),
        D_OWN: copy(shard(zh, core), shard(zh, core), D_OWN, peer),
        D_LEFT: copy(shard(zlft, core), shard(zlft, core), D_LEFT, peer),
        D_RIGHT: copy(shard(zr, core), shard(zr, core), D_RIGHT, peer),
        D_FAR: copy(shard(zf, core), shard(zf, core), D_FAR, peer),
    }
    for number in (AG_RA, AG_LB, AG_RB, AG_LA, D_OWN):
        ag[number].start()

    for k in range(COLS // 128):
        at = slice(k * 128, (k + 1) * 128)
        ratio = w[:, at] / scale
        clipped = jnp.clip(ratio, -8.0, 7.0)
        levels = jnp.floor(clipped + 0.5)
        inside = (ratio >= -8.0) & (ratio <= 7.0)
        ins[:, at] = jnp.where(inside, 1.0, 0.0)
        fac[:, at] = jnp.where(inside, levels - ratio, clipped)

    loads[2].wait()
    for k in range(ROWS // 128):
        at = slice(k * 128, (k + 1) * 128)
        ogt[at, :] = jnp.transpose(og[:, at])
    loads[3].wait()

    def product(j, c, n):
        return jnp.dot(
            ogt[rows_of(j * 2 + c, OWN), :], act[:, n * 256:(n + 1) * 256],
            preferred_element_type=jnp.float32,
        )

    def to_peer(j):
        return copy(
            p_snd.at[rows_of(j, OWN)], p_rcv.at[rows_of(j, OWN)], D_P + j, peer
        )

    @pl.loop(0, 4)
    def _(j):
        for n in range(4):
            p_snd[rows_of(j, OWN), n * 256:(n + 1) * 256] = product(j, other, n).astype(jnp.bfloat16)

        @pl.when(j >= 1)
        def _():
            to_peer(j - 1).start()

    @pl.loop(0, 4)
    def _(j):
        for n in range(4):
            p_own[rows_of(j, OWN), n * 256:(n + 1) * 256] = product(j, core, n)

        @pl.when(j == 0)
        def _():
            to_peer(3).start()

    ag[AG_RA].wait_recv()
    ag[AG_LB].wait_recv()
    ag[AG_FR].start()
    ag[AG_FL].start()

    @pl.loop(0, 4)
    def _(j):
        to_peer(j).wait_recv()
        at = rows_of(j, OWN)
        total = p_own[at, :] + p_rcv[at, :].astype(jnp.float32)
        p_own[at, :] = total
        c_buf[at, :] = total.astype(jnp.bfloat16)

    def c_half(j, h):
        return c_buf.at[rows_of(j * 2 + h, HALF)]

    red = {
        RS_FR: copy(c_half(zf, 0), rs_far.at[0], RS_FR, right),
        RS_FL: copy(c_half(zf, 1), rs_far.at[1], RS_FL, left),
        RS_OR: copy(c_half(zr, 1), rs_own.at[1], RS_OR, right),
        RS_OL: copy(c_half(zlft, 0), rs_own.at[0], RS_OL, left),
        RS_SR: copy(rs_snd.at[0], rs_sum.at[0], RS_SR, right),
        RS_SL: copy(rs_snd.at[1], rs_sum.at[1], RS_SL, left),
    }
    for number in (RS_FR, RS_FL, RS_OR, RS_OL):
        red[number].start()

    ag[AG_RB].wait_recv()
    ag[D_LEFT].start()
    ag[AG_LA].wait_recv()
    ag[D_RIGHT].start()
    ag[AG_FR].wait_recv()
    ag[AG_FL].wait_recv()
    ag[D_FAR].start()
    for number in (D_OWN, D_LEFT, D_RIGHT, D_FAR):
        ag[number].wait_recv()

    def g_half(j, h):
        return g.at[rows_of(j * 2 + h, SUB)]

    ig = {
        Y_FU: copy(g_half(yf, 0), y_far.at[0], Y_FU, up),
        Y_FD: copy(g_half(yf, 1), y_far.at[1], Y_FD, down),
        Y_OU: copy(g_half(yu, 1), y_own.at[1], Y_OU, up),
        Y_OD: copy(g_half(yd, 0), y_own.at[0], Y_OD, down),
        Y_SU: copy(y_snd.at[0], y_sum.at[0], Y_SU, up),
        Y_SD: copy(y_snd.at[1], y_sum.at[1], Y_SD, down),
    }

    def block(t, n):
        return jnp.dot(
            og[rows_of(t, 2 * SUB), :], q[:, n * 256:(n + 1) * 256],
            preferred_element_type=jnp.float32,
        )

    @pl.loop(0, 3)
    def _(k):
        t = jnp.where(k == 0, yf, jnp.where(k == 1, yu, yd))
        for n in range(4):
            g[rows_of(t, 2 * SUB), n * 256:(n + 1) * 256] = block(t, n).astype(jnp.bfloat16)

        @pl.when(k == 0)
        def _():
            ig[Y_FU].start()
            ig[Y_FD].start()

    ig[Y_OU].start()
    ig[Y_OD].start()
    for n in range(4):
        gown[:, n * 256:(n + 1) * 256] = block(y, n)

    red[RS_FR].wait_recv()
    rs_snd[0] = (
        p_own[rows_of(zr * 2, HALF), :] + rs_far[0].astype(jnp.float32)
    ).astype(jnp.bfloat16)
    red[RS_FL].wait_recv()
    rs_snd[1] = (
        p_own[rows_of(zlft * 2 + 1, HALF), :] + rs_far[1].astype(jnp.float32)
    ).astype(jnp.bfloat16)
    red[RS_SR].start()
    red[RS_SL].start()

    ig[Y_FU].wait_recv()
    y_snd[0] = (
        g[rows_of(yu * 2, SUB), :].astype(jnp.float32) + y_far[0].astype(jnp.float32)
    ).astype(jnp.bfloat16)
    ig[Y_FD].wait_recv()
    y_snd[1] = (
        g[rows_of(yd * 2 + 1, SUB), :].astype(jnp.float32) + y_far[1].astype(jnp.float32)
    ).astype(jnp.bfloat16)
    ig[Y_SU].start()
    ig[Y_SD].start()

    for number in (Y_OU, Y_OD, Y_SU, Y_SD):
        ig[number].wait_recv()
    for h in range(2):
        tot[h] = (
            gown[h * SUB:(h + 1) * SUB, :]
            + y_own[h].astype(jnp.float32) + y_sum[h].astype(jnp.float32)
        )
    z_snd[...] = tot[1 - zl].astype(jnp.bfloat16)
    across = copy(z_snd, z_rcv, Z_PAIR, pair)
    across.start()

    for number in (RS_OR, RS_OL, RS_SR, RS_SL):
        red[number].wait_recv()
    parts = jnp.zeros((OWN, 128), jnp.float32)
    for k in range(COLS // 128):
        at = slice(k * 128, (k + 1) * 128)
        both = []
        for h in range(2):
            both.append(
                p_own[rows_of(zh * 2 + h, HALF), at]
                + rs_own[h, :, at].astype(jnp.float32) + rs_sum[h, :, at].astype(jnp.float32)
            )
        summed = jnp.concatenate(both, axis=0)
        wg_out[:, at] = summed * ins[:, at]
        parts = parts + summed * fac[:, at]
    padded = jnp.concatenate([parts, jnp.zeros((256 - OWN, 128), jnp.float32)], axis=0)
    x_snd[...] = jnp.broadcast_to(
        jnp.sum(jnp.transpose(padded), axis=0, keepdims=True) * GRAD_FACTOR, (8, 256)
    )
    sends = [copy(x_snd, x_rcv.at[k], X_SUM + k, crosses[k]) for k in range(3)]
    for send in sends:
        send.start()

    across.wait_recv()
    ig_out[...] = (tot[zl] + z_rcv[...].astype(jnp.float32)).astype(jnp.bfloat16)

    for send in sends:
        send.wait_recv()
    total = x_snd[...] + x_rcv[0] + x_rcv[1] + x_rcv[2]
    sg_out[...] = total[0:1, 0:OWN]

    for group in (ag, red, ig):
        for item in group.values():
            item.wait_send()
    for j in range(4):
        to_peer(j).wait_send()
    across.wait_send()
    for send in sends:
        send.wait_send()


def shards(activations, out_grad, weight, step_size):
    bf16, f32 = jnp.bfloat16, jnp.float32
    hbm = pl.BlockSpec(memory_space=pltpu.HBM)
    vmem = pl.BlockSpec(memory_space=pltpu.VMEM)
    input_grad, weight_grad, step_rows = pl.pallas_call(
        kernel,
        out_shape=(
            jax.ShapeDtypeStruct((SUB, COLS), bf16),
            jax.ShapeDtypeStruct((OWN, COLS), f32),
            jax.ShapeDtypeStruct((1, OWN), f32),
        ),
        in_specs=[hbm] * 4,
        out_specs=(vmem, vmem, vmem),
        scratch_shapes=[
            pltpu.VMEM((TOKENS, COLS), bf16),
            pltpu.VMEM((TOKENS, ROWS), bf16),
            pltpu.VMEM((OWN, COLS), f32),
            pltpu.VMEM((1, ROWS), f32),
            pltpu.VMEM((ROWS, 128), f32),
            pltpu.VMEM((ROWS, TOKENS), bf16),
            pltpu.VMEM((ROWS, COLS), bf16),
            pltpu.VMEM((OWN, COLS), f32),
            pltpu.VMEM((OWN, COLS), f32),
            pltpu.VMEM((4 * OWN, COLS), f32),
            pltpu.VMEM((4 * OWN, COLS), bf16),
            pltpu.VMEM((4 * OWN, COLS), bf16),
            pltpu.VMEM((4 * OWN, COLS), bf16),
            pltpu.VMEM((2, HALF, COLS), bf16),
            pltpu.VMEM((2, HALF, COLS), bf16),
            pltpu.VMEM((2, HALF, COLS), bf16),
            pltpu.VMEM((2, HALF, COLS), bf16),
            pltpu.VMEM((TOKENS, COLS), bf16),
            pltpu.VMEM((2 * SUB, COLS), f32),
            pltpu.VMEM((2, SUB, COLS), bf16),
            pltpu.VMEM((2, SUB, COLS), bf16),
            pltpu.VMEM((2, SUB, COLS), bf16),
            pltpu.VMEM((2, SUB, COLS), bf16),
            pltpu.VMEM((2, SUB, COLS), f32),
            pltpu.VMEM((SUB, COLS), bf16),
            pltpu.VMEM((SUB, COLS), bf16),
            pltpu.VMEM((8, 256), f32),
            pltpu.VMEM((3, 8, 256), f32),
            pltpu.SemaphoreType.DMA((N_COPIES,)),
            pltpu.SemaphoreType.DMA((N_COPIES,)),
            pltpu.SemaphoreType.DMA((4,)),
        ],
        compiler_params=pltpu.CompilerParams(
            collective_id=0, has_side_effects=True, vmem_limit_bytes=60 * 1024 * 1024
        ),
        name="backward",
    )(activations, out_grad, weight[0], step_size)
    return (input_grad, weight_grad[None], step_rows)


def solution(mesh):
    split = Mesh(mesh.devices.reshape(4, 2, 4, 2, 4), ("zh", "core", "y", "zl", "x"))
    in_specs = (P(DP, "x"), P(DP, ROW), P(ROW, DP, "x"), P(ROW, None))
    out_specs = (P(DP + ROW, "x"), P(ROW, DP, "x"), P(ROW, DP))
    return jax.shard_map(
        shards, mesh=split, in_specs=in_specs, out_specs=out_specs, check_vma=False
    )
```

time: 162 us -> 88.2 us (0.54)
  the two profiles are of different devices: /device:TPU:8 before, /device:TPU:1 now
where the time goes in v1:
time: 88.2 us; the launch traced here: 88 us
  Pallas kernels  82.3 us (93%)
  local copies, waits for them, and re-layouts  5.09 us (6%)
    pallas_call x1, Pallas kernels, shards(): pl.pallas_call(kernel, out_shape=(jax.ShapeDtypeStruct((SUB, COLS), bf16)...  82.3 us
    unnamed x3, local copies, waits for them, and re-layouts  5.09 us

profile of v1, /device:TPU:1, one launch (start us, length us, event | category | flops | bytes accessed | tf_op | source)
XLA Modules:
  0.0 88.0 jit_solution(13765447802068577808)
XLA Ops:
  0.6 82.3 %backward.1 = (bf16[128,1024]{1,0:T(8,128)(2,1)}, f32[224,1024]{1,0:T(8,128)}, f32[1,224]{1,0:T(1,128)}) custom-call(bf16[1024,1024]{1,0:T(8,128)(2,1)} %act_hbm.1, bf16[1024,1792]{1,0:T(8,128)(2,1)} %og_hbm.1, f32[224,1024]{1,0:T(8,128)} %bitcast.3, f32[1,1792]{1,0:T(1,128)} %s_hbm.1), custom_call_target="tpu_custom_call" | custom-call | tf_op jit(solution)/shard_map/backward/pallas_call | solution.py:308
  82.9 1.7 %copy.10 = bf16[128,1024]{1,0:T(8,128)(2,1)} copy(bf16[128,1024]{1,0:T(8,128)(2,1)} %get-tuple-element.12) | data formatting | bytes 524288
  84.6 2.2 %copy.11 = f32[1,224,1024]{2,1,0:T(8,128)} copy(f32[1,224,1024]{2,1,0:T(8,128)} %bitcast.2) | data formatting | bytes 1835008
  86.8 1.2 %copy.12 = f32[1,224]{1,0:T(1,128)} copy(f32[1,224]{1,0:T(1,128)} %get-tuple-element.14) | data formatting | bytes 1792

commit v2 on v1

--- a/solution.py
+++ b/solution.py
@@ -301,6 +301,18 @@
         send.wait_send()
 
 
+def store(ig_ref, wg_ref, sg_ref, ig_hbm, wg_hbm, sg_hbm, sems):
+    moves = [
+        pltpu.make_async_copy(wg_ref, wg_hbm, sems.at[0]),
+        pltpu.make_async_copy(ig_ref, ig_hbm, sems.at[1]),
+        pltpu.make_async_copy(sg_ref, sg_hbm, sems.at[2]),
+    ]
+    for move in moves:
+        move.start()
+    for move in moves:
+        move.wait()
+
+
 def shards(activations, out_grad, weight, step_size):
     bf16, f32 = jnp.bfloat16, jnp.float32
     hbm = pl.BlockSpec(memory_space=pltpu.HBM)
@@ -308,9 +320,9 @@
     input_grad, weight_grad, step_rows = pl.pallas_call(
         kernel,
         out_shape=(
-            jax.ShapeDtypeStruct((SUB, COLS), bf16),
-            jax.ShapeDtypeStruct((OWN, COLS), f32),
-            jax.ShapeDtypeStruct((1, OWN), f32),
+            pltpu.VMEM((SUB, COLS), bf16),
+            pltpu.VMEM((OWN, COLS), f32),
+            pltpu.VMEM((1, OWN), f32),
         ),
         in_specs=[hbm] * 4,
         out_specs=(vmem, vmem, vmem),
@@ -348,11 +360,24 @@
             pltpu.SemaphoreType.DMA((4,)),
         ],
         compiler_params=pltpu.CompilerParams(
-            collective_id=0, has_side_effects=True, vmem_limit_bytes=60 * 1024 * 1024
+            collective_id=0, has_side_effects=True, vmem_limit_bytes=60*1024*1024
         ),
         name="backward",
     )(activations, out_grad, weight[0], step_size)
-    return (input_grad, weight_grad[None], step_rows)
+    outs = pl.pallas_call(
+        store,
+        out_shape=(
+            jax.ShapeDtypeStruct((SUB, COLS), bf16),
+            jax.ShapeDtypeStruct((OWN, COLS), f32),
+            jax.ShapeDtypeStruct((1, OWN), f32),
+        ),
+        in_specs=[vmem] * 3,
+        out_specs=(hbm,) * 3,
+        scratch_shapes=[pltpu.SemaphoreType.DMA((3,))],
+        compiler_params=pltpu.CompilerParams(vmem_limit_bytes=4 * 1024 * 1024),
+        name="store",
+    )(input_grad, weight_grad, step_rows)
+    return (outs[0], outs[1][None], outs[2])
 
 
 def solution(mesh):

time: 88.2 us -> 83 us (0.941)
  local copies, waits for them, and re-layouts: 5.09 us -> 0 us
    unnamed x3 -> x0, local copies, waits for them, and re-layouts: 5.09 us -> none
    pallas_call x1 -> x2, Pallas kernels: 82.3 us -> 82.3 us  [the longest x1 81.2 us: shards(): pl.pallas_call(kernel, out_shape=(pltpu.VMEM((SUB, COLS), bf16), pltpu.VM...]
where the time goes in v2:
time: 83 us; the launch traced here: 82.9 us
  Pallas kernels  82.3 us (99%)
    pallas_call x1, Pallas kernels, shards(): pl.pallas_call(kernel, out_shape=(pltpu.VMEM((SUB, COLS), bf16), pltpu.VM...  81.2 us

profile of v2, /device:TPU:1, one launch (start us, length us, event | category | flops | bytes accessed | tf_op | source)
XLA Modules:
  0.0 82.9 jit_solution(3914242794634550595)
XLA Ops:
  0.6 81.2 %backward.1 = (bf16[128,1024]{1,0:T(8,128)(2,1)S(1)}, f32[224,1024]{1,0:T(8,128)S(1)}, f32[1,224]{1,0:T(1,128)S(1)}) custom-call(bf16[1024,1024]{1,0:T(8,128)(2,1)} %act_hbm.1, bf16[1024,1792]{1,0:T(8,128)(2,1)} %og_hbm.1, f32[224,1024]{1,0:T(8,128)} %bitcast.2, f32[1,1792]{1,0:T(1,128)} %s_hbm.1), custom_call_target="tpu_custom_call" | custom-call | tf_op jit(solution)/shard_map/backward/pallas_call | solution.py:320
  81.9 1.0 %store.1 = (bf16[128,1024]{1,0:T(8,128)(2,1)}, f32[224,1024]{1,0:T(8,128)}, f32[1,224]{1,0:T(1,128)}) custom-call(bf16[128,1024]{1,0:T(8,128)(2,1)S(1)} %get-tuple-element.9.ig_ref, f32[224,1024]{1,0:T(8,128)S(1)} %get-tuple-element.10.wg_ref, f32[1,224]{1,0:T(1,128)S(1)} %get-tuple-element.11.sg_ref), custom_call_target="tpu_custom_call" | custom-call | tf_op jit(solution)/shard_map/store/pallas_call | solution.py:367

commit v3 on v2

v3 whole, which is shorter than its diff:
```python
import functools

import jax
import jax.numpy as jnp
from jax import lax
from jax.experimental import pallas as pl
from jax.experimental.pallas import tpu as pltpu
from jax.sharding import Mesh
from jax.sharding import PartitionSpec as P

MESH = pl.DeviceIdType.MESH
D = 4096
DP = ("zh", "core")
ROW = ("y", "zl")
OWN = 224
HALF = 112
COLS = 1024
ROWS = 1792
TOKENS = 1024
SUB = 128
GRAD_FACTOR = 1.0 / (7.0 * D) ** 0.5

AG_RA, AG_RB, AG_LB, AG_LA, AG_FR, AG_FL = range(6)
D_OWN, D_LEFT, D_RIGHT, D_FAR = range(6, 10)
D_P = 10
RS_FAR, RS_ONE, RS_SUM = 14, 16, 18
Y_FP, Y_FM, Y_OP, Y_OM, Y_SP, Y_SM = range(20, 26)
Z_PAIR = 26
X_SUM = 27
T_PAIR = 30
T_X = 31
N_COPIES = 34


def rows_of(index, size):
    return pl.ds(pl.multiple_of(index * size, size), size)


def kernel(
    act_hbm, og_hbm, w_hbm, s_hbm,
    ig_out, wg_out, sg_out,
    act, og, w, s, scol, ogt, ogt_pair, q, fac, ins,
    p_own, p_snd, p_rcv, c_buf,
    rs_far, rs_one, rs_sum, rs_snd, parts,
    g, gown, y_far, y_own, y_sum, y_snd, mine, z_snd, z_rcv,
    x_snd, x_rcv,
    ss, rs, ls,
):
    zh = lax.axis_index("zh")
    core = lax.axis_index("core")
    y = lax.axis_index("y")
    zl = lax.axis_index("zl")
    x = lax.axis_index("x")
    zr, zlft, zf = (zh + 1) % 4, (zh + 3) % 4, (zh + 2) % 4
    right, left = {"zh": zr}, {"zh": zlft}
    zs = (zh + 3 + 2 * zl) % 4
    zo = (zh + 1 + 2 * zl) % 4
    chain = {"zh": zs}
    beside = {"zh": zs, "zl": 1 - zl}
    other = 1 - core
    peer = {"core": other}
    yf = (y + 2) % 4
    pair = {"zl": 1 - zl}
    crosses = [{"x": (x + k) % 4} for k in (1, 2, 3)]
    hp = 1 - zl
    yp = (y + 1 + 2 * hp) % 4
    ym = (y + 3 + 2 * hp) % 4
    way_p, way_m = {"y": yp}, {"y": ym}

    loads = [
        pltpu.make_async_copy(s_hbm, s, ls.at[0]),
        pltpu.make_async_copy(w_hbm, w, ls.at[1]),
        pltpu.make_async_copy(og_hbm, og, ls.at[2]),
        pltpu.make_async_copy(act_hbm, act, ls.at[3]),
    ]
    for load in loads:
        load.start()

    barrier = pltpu.get_barrier_semaphore()
    partners = [right, left, beside, peer, way_p, way_m, pair] + crosses
    for partner in partners:
        pl.semaphore_signal(barrier, inc=1, device_id=partner, device_id_type=MESH)

    def copy(src, dst, number, device):
        return pltpu.make_async_remote_copy(
            src_ref=src, dst_ref=dst, send_sem=ss.at[number], recv_sem=rs.at[number],
            device_id=device, device_id_type=MESH,
        )

    def shard(j, c):
        return q.at[rows_of(j * 2 + c, OWN)]

    def half(j, c, h):
        return q.at[rows_of((j * 2 + c) * 2 + h, HALF)]

    loads[0].wait()
    scol[...] = jnp.transpose(jnp.broadcast_to(s[...], (128, ROWS)))
    loads[1].wait()
    own_at = rows_of(zh * 2 + core, OWN)
    scale = scol[own_at, :]
    for k in range(COLS // 128):
        at = slice(k * 128, (k + 1) * 128)
        ratio = w[:, at] / scale
        levels = jnp.floor(jnp.clip(ratio, -8.0, 7.0) + 0.5)
        q[own_at, at] = (levels * scale).astype(jnp.bfloat16)

    pl.semaphore_wait(barrier, len(partners))

    ag = {
        AG_RA: copy(half(zh, core, 0), half(zh, core, 0), AG_RA, right),
        AG_RB: copy(half(zh, core, 1), half(zh, core, 1), AG_RB, right),
        AG_LB: copy(half(zh, core, 1), half(zh, core, 1), AG_LB, left),
        AG_LA: copy(half(zh, core, 0), half(zh, core, 0), AG_LA, left),
        AG_FR: copy(half(zlft, core, 0), half(zlft, core, 0), AG_FR, right),
        AG_FL: copy(half(zr, core, 1), half(zr, core, 1), AG_FL, left),
        D_OWN: copy(shard(zh, core), shard(zh, core), D_OWN, peer),
        D_LEFT: copy(shard(zlft, core), shard(zlft, core), D_LEFT, peer),
        D_RIGHT: copy(shard(zr, core), shard(zr, core), D_RIGHT, peer),
        D_FAR: copy(shard(zf, core), shard(zf, core), D_FAR, peer),
    }
    for number in (AG_RA, AG_LB, AG_RB, AG_LA, D_OWN):
        ag[number].start()

    loads[2].wait()
    for k in range(ROWS // 128):
        at = slice(k * 128, (k + 1) * 128)
        ogt[at, :] = jnp.transpose(og[:, at])

    for k in range(COLS // 128):
        at = slice(k * 128, (k + 1) * 128)
        ratio = w[:, at] / scale
        clipped = jnp.clip(ratio, -8.0, 7.0)
        levels = jnp.floor(clipped + 0.5)
        inside = (ratio >= -8.0) & (ratio <= 7.0)
        ins[:, at] = jnp.where(inside, 1.0, 0.0)
        fac[:, at] = jnp.where(inside, levels - ratio, clipped)

    quarter = ogt_pair.at[rows_of(x, HALF)]
    turned = copy(ogt.at[rows_of(zo * 4 + x, HALF)], quarter, T_PAIR, pair)
    turned.start()
    loads[3].wait()

    def product(rows, at, c, n):
        return jnp.dot(
            rows[rows_of(at * 2 + c, OWN), :], act[:, n * 256:(n + 1) * 256],
            preferred_element_type=jnp.float32,
        )

    def to_peer(b):
        return copy(
            p_snd.at[rows_of(b, OWN)], p_rcv.at[rows_of(b, OWN)], D_P + b, peer
        )

    @pl.loop(0, 3)
    def _(b):
        dest = jnp.where(b == 0, zf, jnp.where(b == 1, zs, zh))
        for n in range(4):
            at = slice(n * 256, (n + 1) * 256)
            p_snd[rows_of(b, OWN), at] = product(ogt, dest, other, n).astype(jnp.bfloat16)
        for n in range(4):
            at = slice(n * 256, (n + 1) * 256)
            p_own[rows_of(b, OWN), at] = product(ogt, dest, core, n)
        to_peer(b).start()

    turned.wait_recv()
    shares = [copy(quarter, quarter, T_X + k, crosses[k]) for k in range(3)]
    for share in shares:
        share.start()

    ag[AG_RA].wait_recv()
    ag[AG_LB].wait_recv()
    ag[AG_FR].start()
    ag[AG_FL].start()

    for share in shares:
        share.wait_recv()
    for n in range(4):
        at = slice(n * 256, (n + 1) * 256)
        p_snd[3 * OWN:, at] = product(ogt_pair, 0, other, n).astype(jnp.bfloat16)
    for n in range(4):
        at = slice(n * 256, (n + 1) * 256)
        p_own[3 * OWN:, at] = product(ogt_pair, 0, core, n)
    to_peer(3).start()

    @pl.loop(0, 4)
    def _(b):
        to_peer(b).wait_recv()
        at = rows_of(b, OWN)
        total = p_own[at, :] + p_rcv[at, :].astype(jnp.float32)
        p_own[at, :] = total
        c_buf[at, :] = total.astype(jnp.bfloat16)

    def c_half(b, h):
        return c_buf.at[(2 * b + h) * HALF:(2 * b + h + 1) * HALF]

    far = [copy(c_half(0, h), rs_far.at[h], RS_FAR + h, chain) for h in range(2)]
    one = [copy(c_half(3, h), rs_one.at[h], RS_ONE + h, beside) for h in range(2)]
    whole = [copy(rs_snd.at[h], rs_sum.at[h], RS_SUM + h, chain) for h in range(2)]

    ag[AG_RB].wait_recv()
    ag[D_LEFT].start()
    ag[AG_LA].wait_recv()
    ag[D_RIGHT].start()
    ag[AG_FR].wait_send()
    ag[AG_FL].wait_send()
    for item in far + one:
        item.start()
    ag[AG_FR].wait_recv()
    ag[AG_FL].wait_recv()
    ag[D_FAR].start()
    for number in (D_OWN, D_LEFT, D_RIGHT, D_FAR):
        ag[number].wait_recv()

    def g_half(j, h):
        return g.at[rows_of(j * 2 + h, SUB)]

    ig = {
        Y_FP: copy(g_half(yf, hp), y_far.at[0], Y_FP, way_p),
        Y_FM: copy(g_half(yf, zl), y_far.at[1], Y_FM, way_m),
        Y_OP: copy(g_half(ym, hp), y_own.at[0], Y_OP, way_m),
        Y_OM: copy(g_half(yp, zl), y_own.at[1], Y_OM, way_p),
        Y_SP: copy(y_snd.at[0], y_sum.at[0], Y_SP, way_p),
        Y_SM: copy(y_snd.at[1], y_sum.at[1], Y_SM, way_m),
    }

    def block(t, n):
        return jnp.dot(
            og[rows_of(t, 2 * SUB), :], q[:, n * 256:(n + 1) * 256],
            preferred_element_type=jnp.float32,
        )

    @pl.loop(0, 3)
    def _(k):
        t = jnp.where(k == 0, yf, jnp.where(k == 1, ym, yp))
        for n in range(4):
            g[rows_of(t, 2 * SUB), n * 256:(n + 1) * 256] = block(t, n).astype(jnp.bfloat16)

        @pl.when(k == 0)
        def _():
            ig[Y_FP].start()
            ig[Y_FM].start()

        @pl.when(k == 1)
        def _():
            ig[Y_OP].start()

    for n in range(4):
        gown[:, n * 256:(n + 1) * 256] = block(y, n)

    def middle(h):
        far[h].wait_recv()
        rs_snd[h] = (
            p_own[OWN + h * HALF:OWN + (h + 1) * HALF, :] + rs_far[h].astype(jnp.float32)
        ).astype(jnp.bfloat16)
        whole[h].start()

    middle(0)
    ig[Y_FP].wait_recv()
    y_snd[0] = (
        g[rows_of(yp * 2 + hp, SUB), :].astype(jnp.float32) + y_far[0].astype(jnp.float32)
    ).astype(jnp.bfloat16)
    ig[Y_SP].start()
    ig[Y_OM].start()
    ig[Y_FM].wait_recv()
    y_snd[1] = (
        g[rows_of(ym * 2 + zl, SUB), :].astype(jnp.float32) + y_far[1].astype(jnp.float32)
    ).astype(jnp.bfloat16)
    ig[Y_SM].start()
    middle(1)

    ig[Y_OP].wait_recv()
    ig[Y_SP].wait_recv()
    z_snd[...] = (
        gown[rows_of(hp, SUB), :] + y_own[0].astype(jnp.float32) + y_sum[0].astype(jnp.float32)
    ).astype(jnp.bfloat16)
    across = copy(z_snd, z_rcv, Z_PAIR, pair)
    across.start()
    ig[Y_OM].wait_recv()
    ig[Y_SM].wait_recv()
    mine[...] = (
        gown[rows_of(zl, SUB), :] + y_own[1].astype(jnp.float32) + y_sum[1].astype(jnp.float32)
    )

    def finish(h):
        one[h].wait_recv()
        whole[h].wait_recv()
        rows = slice(h * HALF, (h + 1) * HALF)
        part = jnp.zeros((HALF, 128), jnp.float32)
        for k in range(COLS // 128):
            at = slice(k * 128, (k + 1) * 128)
            summed = (
                p_own[2 * OWN + h * HALF:2 * OWN + (h + 1) * HALF, at]
                + rs_one[h, :, at].astype(jnp.float32) + rs_sum[h, :, at].astype(jnp.float32)
            )
            wg_out[rows, at] = summed * ins[rows, at]
            part = part + summed * fac[rows, at]
        parts[rows, :] = part

    parts[OWN:, :] = jnp.zeros((256 - OWN, 128), jnp.float32)
    finish(0)
    across.wait_recv()
    ig_out[...] = (mine[...] + z_rcv[...].astype(jnp.float32)).astype(jnp.bfloat16)
    finish(1)
    x_snd[...] = jnp.broadcast_to(
        jnp.sum(jnp.transpose(parts[...]), axis=0, keepdims=True) * GRAD_FACTOR, (8, 256)
    )
    sends = [copy(x_snd, x_rcv.at[k], X_SUM + k, crosses[k]) for k in range(3)]
    for send in sends:
        send.start()

    for number in ag:
        if number not in (AG_FR, AG_FL):
            ag[number].wait_send()
    for item in list(ig.values()) + far + one + whole + shares + [turned, across]:
        item.wait_send()
    for b in range(4):
        to_peer(b).wait_send()

    for send in sends:
        send.wait_recv()
    total = x_snd[...] + x_rcv[0] + x_rcv[1] + x_rcv[2]
    sg_out[...] = total[0:1, 0:OWN]
    for send in sends:
        send.wait_send()


def store(ig_ref, wg_ref, sg_ref, ig_hbm, wg_hbm, sg_hbm, sems):
    moves = [
        pltpu.make_async_copy(wg_ref, wg_hbm, sems.at[0]),
        pltpu.make_async_copy(ig_ref, ig_hbm, sems.at[1]),
        pltpu.make_async_copy(sg_ref, sg_hbm, sems.at[2]),
    ]
    for move in moves:
        move.start()
    for move in moves:
        move.wait()


def shards(activations, out_grad, weight, step_size):
    bf16, f32 = jnp.bfloat16, jnp.float32
    hbm = pl.BlockSpec(memory_space=pltpu.HBM)
    vmem = pl.BlockSpec(memory_space=pltpu.VMEM)
    input_grad, weight_grad, step_rows = pl.pallas_call(
        kernel,
        out_shape=(
            pltpu.VMEM((SUB, COLS), bf16),
            pltpu.VMEM((OWN, COLS), f32),
            pltpu.VMEM((1, OWN), f32),
        ),
        in_specs=[hbm] * 4,
        out_specs=(vmem, vmem, vmem),
        scratch_shapes=[
            pltpu.VMEM((TOKENS, COLS), bf16),
            pltpu.VMEM((TOKENS, ROWS), bf16),
            pltpu.VMEM((OWN, COLS), f32),
            pltpu.VMEM((1, ROWS), f32),
            pltpu.VMEM((ROWS, 128), f32),
            pltpu.VMEM((ROWS, TOKENS), bf16),
            pltpu.VMEM((2 * OWN, TOKENS), bf16),
            pltpu.VMEM((ROWS, COLS), bf16),
            pltpu.VMEM((OWN, COLS), f32),
            pltpu.VMEM((OWN, COLS), f32),
            pltpu.VMEM((4 * OWN, COLS), f32),
            pltpu.VMEM((4 * OWN, COLS), bf16),
            pltpu.VMEM((4 * OWN, COLS), bf16),
            pltpu.VMEM((4 * OWN, COLS), bf16),
            pltpu.VMEM((2, HALF, COLS), bf16),
            pltpu.VMEM((2, HALF, COLS), bf16),
            pltpu.VMEM((2, HALF, COLS), bf16),
            pltpu.VMEM((2, HALF, COLS), bf16),
            pltpu.VMEM((256, 128), f32),
            pltpu.VMEM((TOKENS, COLS), bf16),
            pltpu.VMEM((2 * SUB, COLS), f32),
            pltpu.VMEM((2, SUB, COLS), bf16),
            pltpu.VMEM((2, SUB, COLS), bf16),
            pltpu.VMEM((2, SUB, COLS), bf16),
            pltpu.VMEM((2, SUB, COLS), bf16),
            pltpu.VMEM((SUB, COLS), f32),
            pltpu.VMEM((SUB, COLS), bf16),
            pltpu.VMEM((SUB, COLS), bf16),
            pltpu.VMEM((8, 256), f32),
            pltpu.VMEM((3, 8, 256), f32),
            pltpu.SemaphoreType.DMA((N_COPIES,)),
            pltpu.SemaphoreType.DMA((N_COPIES,)),
            pltpu.SemaphoreType.DMA((4,)),
        ],
        compiler_params=pltpu.CompilerParams(
            collective_id=0, has_side_effects=True, vmem_limit_bytes=60*1024*1024
        ),
        name="backward",
    )(activations, out_grad, weight[0], step_size)
    outs = pl.pallas_call(
        store,
        out_shape=(
            jax.ShapeDtypeStruct((SUB, COLS), bf16),
            jax.ShapeDtypeStruct((OWN, COLS), f32),
            jax.ShapeDtypeStruct((1, OWN), f32),
        ),
        in_specs=[vmem] * 3,
        out_specs=(hbm,) * 3,
        scratch_shapes=[pltpu.SemaphoreType.DMA((3,))],
        compiler_params=pltpu.CompilerParams(vmem_limit_bytes=4 * 1024 * 1024),
        name="store",
    )(input_grad, weight_grad, step_rows)
    return (outs[0], outs[1][None], outs[2])


def solution(mesh):
    split = Mesh(mesh.devices.reshape(4, 2, 4, 2, 4), ("zh", "core", "y", "zl", "x"))
    in_specs = (P(DP, "x"), P(DP, ROW), P(ROW, DP, "x"), P(ROW, None))
    out_specs = (P(DP + ROW, "x"), P(ROW, DP, "x"), P(ROW, DP))
    return jax.shard_map(
        shards, mesh=split, in_specs=in_specs, out_specs=out_specs, check_vma=False
    )
```

time: 83 us -> 88.5 us (1.066)
  the two profiles are of different devices: /device:TPU:1 before, /device:TPU:8 now
where the time goes in v3:
time: 88.5 us; the launch traced here: 88.1 us
  Pallas kernels  87.4 us (99%)
    pallas_call x1, Pallas kernels, shards(): pl.pallas_call(kernel, out_shape=(pltpu.VMEM((SUB, COLS), bf16), pltpu.VM...  86.4 us

profile of v3, /device:TPU:8, one launch (start us, length us, event | category | flops | bytes accessed | tf_op | source)
XLA Modules:
  0.0 88.1 jit_solution(8629085562326260172)
XLA Ops:
  0.6 86.4 %backward.1 = (bf16[128,1024]{1,0:T(8,128)(2,1)S(1)}, f32[224,1024]{1,0:T(8,128)S(1)}, f32[1,224]{1,0:T(1,128)S(1)}) custom-call(bf16[1024,1024]{1,0:T(8,128)(2,1)} %act_hbm.1, bf16[1024,1792]{1,0:T(8,128)(2,1)} %og_hbm.1, f32[224,1024]{1,0:T(8,128)} %bitcast.2, f32[1,1792]{1,0:T(1,128)} %s_hbm.1), custom_call_target="tpu_custom_call" | custom-call | tf_op jit(solution)/shard_map/backward/pallas_call | solution.py:343
  87.1 1.0 %store.1 = (bf16[128,1024]{1,0:T(8,128)(2,1)}, f32[224,1024]{1,0:T(8,128)}, f32[1,224]{1,0:T(1,128)}) custom-call(bf16[128,1024]{1,0:T(8,128)(2,1)S(1)} %get-tuple-element.9.ig_ref, f32[224,1024]{1,0:T(8,128)S(1)} %get-tuple-element.10.wg_ref, f32[1,224]{1,0:T(1,128)S(1)} %get-tuple-element.11.sg_ref), custom_call_target="tpu_custom_call" | custom-call | tf_op jit(solution)/shard_map/store/pallas_call | solution.py:392

commit v4 on v3

--- a/solution.py
+++ b/solution.py
@@ -20,8 +20,8 @@
 SUB = 128
 GRAD_FACTOR = 1.0 / (7.0 * D) ** 0.5
 
-AG_RA, AG_RB, AG_LB, AG_LA, AG_FR, AG_FL = range(6)
-D_OWN, D_LEFT, D_RIGHT, D_FAR = range(6, 10)
+AG_OWN, AG_FWD, AG_ONE = 0, 2, 4
+D_OWN, D_NEAR, D_FAR, D_BESIDE = range(6, 10)
 D_P = 10
 RS_FAR, RS_ONE, RS_SUM = 14, 16, 18
 Y_FP, Y_FM, Y_OP, Y_OM, Y_SP, Y_SM = range(20, 26)
@@ -51,11 +51,10 @@
     y = lax.axis_index("y")
     zl = lax.axis_index("zl")
     x = lax.axis_index("x")
-    zr, zlft, zf = (zh + 1) % 4, (zh + 3) % 4, (zh + 2) % 4
-    right, left = {"zh": zr}, {"zh": zlft}
+    zf = (zh + 2) % 4
     zs = (zh + 3 + 2 * zl) % 4
     zo = (zh + 1 + 2 * zl) % 4
-    chain = {"zh": zs}
+    chain, back = {"zh": zs}, {"zh": zo}
     beside = {"zh": zs, "zl": 1 - zl}
     other = 1 - core
     peer = {"core": other}
@@ -73,11 +72,11 @@
         pltpu.make_async_copy(og_hbm, og, ls.at[2]),
         pltpu.make_async_copy(act_hbm, act, ls.at[3]),
     ]
-    for load in loads:
-        load.start()
+    loads[0].start()
+    loads[1].start()
 
     barrier = pltpu.get_barrier_semaphore()
-    partners = [right, left, beside, peer, way_p, way_m, pair] + crosses
+    partners = [chain, back, beside, peer, way_p, way_m, pair] + crosses
     for partner in partners:
         pl.semaphore_signal(barrier, inc=1, device_id=partner, device_id_type=MESH)
 
@@ -87,13 +86,15 @@
             device_id=device, device_id_type=MESH,
         )
 
-    def shard(j, c):
-        return q.at[rows_of(j * 2 + c, OWN)]
-
-    def half(j, c, h):
-        return q.at[rows_of((j * 2 + c) * 2 + h, HALF)]
+    def shard(j):
+        return q.at[rows_of(j * 2 + core, OWN)]
+
+    def half(j, h):
+        return q.at[rows_of((j * 2 + core) * 2 + h, HALF)]
 
     loads[0].wait()
+    loads[2].start()
+    loads[3].start()
     scol[...] = jnp.transpose(jnp.broadcast_to(s[...], (128, ROWS)))
     loads[1].wait()
     own_at = rows_of(zh * 2 + core, OWN)
@@ -106,25 +107,29 @@
 
     pl.semaphore_wait(barrier, len(partners))
 
-    ag = {
-        AG_RA: copy(half(zh, core, 0), half(zh, core, 0), AG_RA, right),
-        AG_RB: copy(half(zh, core, 1), half(zh, core, 1), AG_RB, right),
-        AG_LB: copy(half(zh, core, 1), half(zh, core, 1), AG_LB, left),
-        AG_LA: copy(half(zh, core, 0), half(zh, core, 0), AG_LA, left),
-        AG_FR: copy(half(zlft, core, 0), half(zlft, core, 0), AG_FR, right),
-        AG_FL: copy(half(zr, core, 1), half(zr, core, 1), AG_FL, left),
-        D_OWN: copy(shard(zh, core), shard(zh, core), D_OWN, peer),
-        D_LEFT: copy(shard(zlft, core), shard(zlft, core), D_LEFT, peer),
-        D_RIGHT: copy(shard(zr, core), shard(zr, core), D_RIGHT, peer),
-        D_FAR: copy(shard(zf, core), shard(zf, core), D_FAR, peer),
+    own = [copy(half(zh, h), half(zh, h), AG_OWN + h, back) for h in range(2)]
+    fwd = [copy(half(zs, h), half(zs, h), AG_FWD + h, back) for h in range(2)]
+    aside = [copy(half(zh, h), half(zf, h), AG_ONE + h, beside) for h in range(2)]
+    swap = {
+        D_OWN: copy(shard(zh), shard(zh), D_OWN, peer),
+        D_NEAR: copy(shard(zs), shard(zs), D_NEAR, peer),
+        D_FAR: copy(shard(zf), shard(zf), D_FAR, peer),
+        D_BESIDE: copy(shard(zo), shard(zo), D_BESIDE, peer),
     }
-    for number in (AG_RA, AG_LB, AG_RB, AG_LA, D_OWN):
-        ag[number].start()
+    own[0].start()
+    aside[0].start()
+    aside[1].start()
+    swap[D_OWN].start()
 
     loads[2].wait()
     for k in range(ROWS // 128):
         at = slice(k * 128, (k + 1) * 128)
         ogt[at, :] = jnp.transpose(og[:, at])
+
+    quarter = ogt_pair.at[rows_of(x, HALF)]
+    turned = copy(ogt.at[rows_of(zo * 4 + x, HALF)], quarter, T_PAIR, pair)
+    turned.start()
+    own[1].start()
 
     for k in range(COLS // 128):
         at = slice(k * 128, (k + 1) * 128)
@@ -135,14 +140,11 @@
         ins[:, at] = jnp.where(inside, 1.0, 0.0)
         fac[:, at] = jnp.where(inside, levels - ratio, clipped)
 
-    quarter = ogt_pair.at[rows_of(x, HALF)]
-    turned = copy(ogt.at[rows_of(zo * 4 + x, HALF)], quarter, T_PAIR, pair)
-    turned.start()
     loads[3].wait()
 
-    def product(rows, at, c, n):
+    def product(at, c, n):
         return jnp.dot(
-            rows[rows_of(at * 2 + c, OWN), :], act[:, n * 256:(n + 1) * 256],
+            ogt[rows_of(at * 2 + c, OWN), :], act[:, n * 256:(n + 1) * 256],
             preferred_element_type=jnp.float32,
         )
 
@@ -156,40 +158,26 @@
         dest = jnp.where(b == 0, zf, jnp.where(b == 1, zs, zh))
         for n in range(4):
             at = slice(n * 256, (n + 1) * 256)
-            p_snd[rows_of(b, OWN), at] = product(ogt, dest, other, n).astype(jnp.bfloat16)
+            p_snd[rows_of(b, OWN), at] = product(dest, other, n).astype(jnp.bfloat16)
         for n in range(4):
             at = slice(n * 256, (n + 1) * 256)
-            p_own[rows_of(b, OWN), at] = product(ogt, dest, core, n)
+            p_own[rows_of(b, OWN), at] = product(dest, core, n)
         to_peer(b).start()
 
-    turned.wait_recv()
-    shares = [copy(quarter, quarter, T_X + k, crosses[k]) for k in range(3)]
-    for share in shares:
-        share.start()
-
-    ag[AG_RA].wait_recv()
-    ag[AG_LB].wait_recv()
-    ag[AG_FR].start()
-    ag[AG_FL].start()
-
-    for share in shares:
-        share.wait_recv()
-    for n in range(4):
-        at = slice(n * 256, (n + 1) * 256)
-        p_snd[3 * OWN:, at] = product(ogt_pair, 0, other, n).astype(jnp.bfloat16)
-    for n in range(4):
-        at = slice(n * 256, (n + 1) * 256)
-        p_own[3 * OWN:, at] = product(ogt_pair, 0, core, n)
-    to_peer(3).start()
-
-    @pl.loop(0, 4)
-    def _(b):
+    def chip_sum(b):
         to_peer(b).wait_recv()
         at = rows_of(b, OWN)
         total = p_own[at, :] + p_rcv[at, :].astype(jnp.float32)
         p_own[at, :] = total
         c_buf[at, :] = total.astype(jnp.bfloat16)
 
+    own[0].wait_recv()
+    fwd[0].start()
+
+    @pl.loop(0, 3)
+    def _(b):
+        chip_sum(b)
+
     def c_half(b, h):
         return c_buf.at[(2 * b + h) * HALF:(2 * b + h + 1) * HALF]
 
@@ -197,19 +185,42 @@
     one = [copy(c_half(3, h), rs_one.at[h], RS_ONE + h, beside) for h in range(2)]
     whole = [copy(rs_snd.at[h], rs_sum.at[h], RS_SUM + h, chain) for h in range(2)]
 
-    ag[AG_RB].wait_recv()
-    ag[D_LEFT].start()
-    ag[AG_LA].wait_recv()
-    ag[D_RIGHT].start()
-    ag[AG_FR].wait_send()
-    ag[AG_FL].wait_send()
-    for item in far + one:
+    for item in far:
         item.start()
-    ag[AG_FR].wait_recv()
-    ag[AG_FL].wait_recv()
-    ag[D_FAR].start()
-    for number in (D_OWN, D_LEFT, D_RIGHT, D_FAR):
-        ag[number].wait_recv()
+
+    turned.wait_recv()
+    shares = [copy(quarter, quarter, T_X + k, crosses[k]) for k in range(3)]
+    for share in shares:
+        share.start()
+    own[1].wait_recv()
+    fwd[1].start()
+    swap[D_NEAR].start()
+
+    for share in shares:
+        share.wait_recv()
+    turned.wait_send()
+    ogt[rows_of(zo, 2 * OWN), :] = ogt_pair[...]
+    for n in range(4):
+        at = slice(n * 256, (n + 1) * 256)
+        p_snd[3 * OWN:, at] = product(zo, other, n).astype(jnp.bfloat16)
+    for n in range(4):
+        at = slice(n * 256, (n + 1) * 256)
+        p_own[3 * OWN:, at] = product(zo, core, n)
+    to_peer(3).start()
+    for k in range(ROWS // 128):
+        at = slice(k * 128, (k + 1) * 128)
+        og[:, at] = jnp.transpose(ogt[at, :])
+    chip_sum(3)
+
+    one[0].start()
+    for item in aside:
+        item.wait_recv()
+    swap[D_BESIDE].start()
+    fwd[0].wait_recv()
+    fwd[1].wait_recv()
+    swap[D_FAR].start()
+    for item in swap.values():
+        item.wait_recv()
 
     def g_half(j, h):
         return g.at[rows_of(j * 2 + h, SUB)]
@@ -261,12 +272,14 @@
     ).astype(jnp.bfloat16)
     ig[Y_SP].start()
     ig[Y_OM].start()
+
     ig[Y_FM].wait_recv()
     y_snd[1] = (
         g[rows_of(ym * 2 + zl, SUB), :].astype(jnp.float32) + y_far[1].astype(jnp.float32)
     ).astype(jnp.bfloat16)
     ig[Y_SM].start()
     middle(1)
+    one[1].start()
 
     ig[Y_OP].wait_recv()
     ig[Y_SP].wait_recv()
@@ -282,8 +295,8 @@
     )
 
     def finish(h):
+        whole[h].wait_recv()
         one[h].wait_recv()
-        whole[h].wait_recv()
         rows = slice(h * HALF, (h + 1) * HALF)
         part = jnp.zeros((HALF, 128), jnp.float32)
         for k in range(COLS // 128):
@@ -298,8 +311,6 @@
 
     parts[OWN:, :] = jnp.zeros((256 - OWN, 128), jnp.float32)
     finish(0)
-    across.wait_recv()
-    ig_out[...] = (mine[...] + z_rcv[...].astype(jnp.float32)).astype(jnp.bfloat16)
     finish(1)
     x_snd[...] = jnp.broadcast_to(
         jnp.sum(jnp.transpose(parts[...]), axis=0, keepdims=True) * GRAD_FACTOR, (8, 256)
@@ -308,10 +319,10 @@
     for send in sends:
         send.start()
 
-    for number in ag:
-        if number not in (AG_FR, AG_FL):
-            ag[number].wait_send()
-    for item in list(ig.values()) + far + one + whole + shares + [turned, across]:
+    across.wait_recv()
+    ig_out[...] = (mine[...] + z_rcv[...].astype(jnp.float32)).astype(jnp.bfloat16)
+
+    for item in list(swap.values()) + list(ig.values()) + own + fwd + aside + far + one + whole + shares + [across]:
         item.wait_send()
     for b in range(4):
         to_peer(b).wait_send()

time: 88.5 us -> 75.6 us (0.85)
  Pallas kernels: 87.4 us -> 73.7 us
    pallas_call x1, Pallas kernels: 86.4 us -> 72.7 us  [shards(): pl.pallas_call(kernel, out_shape=(pltpu.VMEM((SUB, COLS), bf16), pltpu.VM...]
where the time goes in v4:
time: 75.6 us; the launch traced here: 74.4 us
  Pallas kernels  73.7 us (97%)
    pallas_call x1, Pallas kernels, shards(): pl.pallas_call(kernel, out_shape=(pltpu.VMEM((SUB, COLS), bf16), pltpu.VM...  72.7 us

profile of v4, /device:TPU:8, one launch (start us, length us, event | category | flops | bytes accessed | tf_op | source)
XLA Modules:
  0.0 74.4 jit_solution(13601445819346979428)
XLA Ops:
  0.6 72.7 %backward.1 = (bf16[128,1024]{1,0:T(8,128)(2,1)S(1)}, f32[224,1024]{1,0:T(8,128)S(1)}, f32[1,224]{1,0:T(1,128)S(1)}) custom-call(bf16[1024,1024]{1,0:T(8,128)(2,1)} %act_hbm.1, bf16[1024,1792]{1,0:T(8,128)(2,1)} %og_hbm.1, f32[224,1024]{1,0:T(8,128)} %bitcast.2, f32[1,1792]{1,0:T(1,128)} %s_hbm.1), custom_call_target="tpu_custom_call" | custom-call | tf_op jit(solution)/shard_map/backward/pallas_call | solution.py:354
  73.3 1.0 %store.1 = (bf16[128,1024]{1,0:T(8,128)(2,1)}, f32[224,1024]{1,0:T(8,128)}, f32[1,224]{1,0:T(1,128)}) custom-call(bf16[128,1024]{1,0:T(8,128)(2,1)S(1)} %get-tuple-element.9.ig_ref, f32[224,1024]{1,0:T(8,128)S(1)} %get-tuple-element.10.wg_ref, f32[1,224]{1,0:T(1,128)S(1)} %get-tuple-element.11.sg_ref), custom_call_target="tpu_custom_call" | custom-call | tf_op jit(solution)/shard_map/store/pallas_call | solution.py:403

commit v5 on v4

v5 whole, which is shorter than its diff:
```python
import functools

import jax
import jax.numpy as jnp
from jax import lax
from jax.experimental import pallas as pl
from jax.experimental.pallas import tpu as pltpu
from jax.sharding import Mesh
from jax.sharding import PartitionSpec as P

MESH = pl.DeviceIdType.MESH
D = 4096
DP = ("zh", "core")
ROW = ("y", "zl")
OWN = 224
HALF = 112
COLS = 1024
ROWS = 1792
TOKENS = 1024
SUB = 128
CHUNKS = ((0, 112), (112, 192), (192, 224))
GRAD_FACTOR = 1.0 / (7.0 * D) ** 0.5

S_MAIN, S_P, S_Y, S_SHARE, S_TURN, S_X, N_SEND = range(7)
(
    R_OWN, _, R_FWD, R_ASIDE, R_SWAP, R_P, R_P3, R_FAR, _, R_SUM, _, R_ONE, _, _,
    R_FP, R_FM, R_PP, R_MM, R_Z, R_X, R_TURN, R_SHARE, N_RECV,
) = range(23)


def rows_of(index, size):
    return pl.ds(pl.multiple_of(index * size, size), size)


def kernel(
    act_hbm, og_hbm, w_hbm, s_hbm,
    ig_out, wg_out, sg_out,
    act, og, w, s, scol, ogt, ogt_pair, q, fac, ins,
    p_own, p_snd, p_rcv, c_buf,
    rs_far, rs_one, rs_sum, rs_snd, parts,
    g, gown, y_far, y_own, y_sum, y_snd, mine, z_snd, z_rcv,
    x_snd, x_rcv,
    ss, rs, ls,
):
    zh = lax.axis_index("zh")
    core = lax.axis_index("core")
    y = lax.axis_index("y")
    zl = lax.axis_index("zl")
    x = lax.axis_index("x")
    zf = (zh + 2) % 4
    zs = (zh + 3 + 2 * zl) % 4
    zo = (zh + 1 + 2 * zl) % 4
    chain, back = {"zh": zs}, {"zh": zo}
    beside = {"zh": zs, "zl": 1 - zl}
    other = 1 - core
    peer = {"core": other}
    yf = (y + 2) % 4
    pair = {"zl": 1 - zl}
    crosses = [{"x": (x + k) % 4} for k in (2, 1, 3)]
    hp = 1 - zl
    yp = (y + 1 + 2 * hp) % 4
    ym = (y + 3 + 2 * hp) % 4
    way_p, way_m = {"y": yp}, {"y": ym}

    loads = [
        pltpu.make_async_copy(s_hbm, s, ls.at[0]),
        pltpu.make_async_copy(w_hbm.at[0:HALF], w.at[0:HALF], ls.at[1]),
        pltpu.make_async_copy(w_hbm.at[HALF:OWN], w.at[HALF:OWN], ls.at[2]),
        pltpu.make_async_copy(og_hbm, og, ls.at[3]),
        pltpu.make_async_copy(act_hbm, act, ls.at[4]),
    ]
    barrier = pltpu.get_barrier_semaphore()
    partners = [chain, back, beside, peer, way_p, way_m, pair] + crosses
    for partner in partners:
        pl.semaphore_signal(barrier, inc=1, device_id=partner, device_id_type=MESH)
    for load in loads[:3]:
        load.start()

    def copy(src, dst, sender, receiver, device):
        return pltpu.make_async_remote_copy(
            src_ref=src, dst_ref=dst, send_sem=ss.at[sender], recv_sem=rs.at[receiver],
            device_id=device, device_id_type=MESH,
        )

    def wait_received(receiver, rows):
        copy(q.at[0:rows], q.at[0:rows], S_MAIN, receiver, peer).wait_recv()

    def wait_sent(sender, rows):
        copy(q.at[0:rows], q.at[0:rows], sender, R_SWAP, peer).wait_send()

    def shard(j):
        return q.at[rows_of(j * 2 + core, OWN)]

    def half(j, h):
        return q.at[rows_of((j * 2 + core) * 2 + h, HALF)]

    first_row = (zh * 2 + core) * OWN
    tile = jnp.minimum(first_row // 128, (ROWS - 3 * 128) // 128)
    loads[0].wait()
    scol[...] = jnp.transpose(
        jnp.broadcast_to(s[:, pl.ds(pl.multiple_of(tile * 128, 128), 3 * 128)], (128, 3 * 128))
    )
    scale_at = first_row - tile * 128

    def quantize(h):
        rows = slice(h * HALF, (h + 1) * HALF)
        scale = scol[pl.ds(pl.multiple_of(scale_at + h * HALF, 16), HALF), :]
        for k in range(COLS // 128):
            at = slice(k * 128, (k + 1) * 128)
            levels = jnp.floor(jnp.clip(w[rows, at] / scale, -8.0, 7.0) + 0.5)
            q[rows_of((zh * 2 + core) * 2 + h, HALF), at] = (levels * scale).astype(jnp.bfloat16)

    loads[1].wait()
    quantize(0)
    pl.semaphore_wait(barrier, len(partners))

    own = [copy(half(zh, h), half(zh, h), S_MAIN, R_OWN + h, back) for h in range(2)]
    fwd = [copy(half(zs, h), half(zs, h), S_MAIN, R_FWD, back) for h in range(2)]
    aside = [copy(half(zh, h), half(zf, h), S_MAIN, R_ASIDE, beside) for h in range(2)]

    def swap(j):
        return copy(shard(j), shard(j), S_MAIN, R_SWAP, peer)

    own[0].start()
    aside[0].start()
    loads[3].start()
    loads[4].start()
    loads[2].wait()
    quantize(1)

    loads[3].wait()
    aside[1].start()
    swap(zh).start()
    for k in range(ROWS // 128):
        at = slice(k * 128, (k + 1) * 128)
        ogt[at, :] = jnp.transpose(og[:, at])

    quarter = ogt_pair.at[rows_of(x, HALF)]
    turned = copy(ogt.at[rows_of(zo * 4 + x, HALF)], quarter, S_TURN, R_TURN, pair)
    turned.start()
    own[1].start()

    scale = scol[pl.ds(pl.multiple_of(scale_at, 16), OWN), :]
    for k in range(COLS // 128):
        at = slice(k * 128, (k + 1) * 128)
        ratio = w[:, at] / scale
        clipped = jnp.clip(ratio, -8.0, 7.0)
        levels = jnp.floor(clipped + 0.5)
        inside = (ratio >= -8.0) & (ratio <= 7.0)
        ins[:, at] = jnp.where(inside, 1.0, 0.0)
        fac[:, at] = jnp.where(inside, levels - ratio, clipped)

    loads[4].wait()

    def product(at, c, n):
        return jnp.dot(
            ogt[rows_of(at * 2 + c, OWN), :], act[:, n * 256:(n + 1) * 256],
            preferred_element_type=jnp.float32,
        )

    def to_peer(b, receiver):
        return copy(
            p_snd.at[rows_of(b, OWN)], p_rcv.at[rows_of(b, OWN)], S_P, receiver, peer
        )

    @pl.loop(0, 3)
    def _(b):
        dest = jnp.where(b == 0, zf, jnp.where(b == 1, zs, zh))
        for n in range(4):
            at = slice(n * 256, (n + 1) * 256)
            p_snd[rows_of(b, OWN), at] = product(dest, other, n).astype(jnp.bfloat16)
        for n in range(4):
            at = slice(n * 256, (n + 1) * 256)
            p_own[rows_of(b, OWN), at] = product(dest, core, n)
        to_peer(b, R_P).start()

    def chip_sum(b):
        at = rows_of(b, OWN)
        total = p_own[at, :] + p_rcv[at, :].astype(jnp.float32)
        p_own[at, :] = total
        c_buf[at, :] = total.astype(jnp.bfloat16)

    own[0].wait_recv()
    fwd[0].start()

    wait_received(R_P, 3 * OWN)

    @pl.loop(0, 3)
    def _(b):
        chip_sum(b)

    def c_half(b, h):
        return c_buf.at[(2 * b + h) * HALF:(2 * b + h + 1) * HALF]

    far = [copy(c_half(0, h), rs_far.at[h], S_MAIN, R_FAR + h, chain) for h in range(2)]
    one = [
        copy(c_buf.at[3 * OWN + i:3 * OWN + j], rs_one.at[i:j], S_P, R_ONE + n, beside)
        for n, (i, j) in enumerate(CHUNKS)
    ]
    whole = [copy(rs_snd.at[h], rs_sum.at[h * HALF:(h + 1) * HALF], S_P, R_SUM + h, chain) for h in range(2)]

    for item in far:
        item.start()

    turned.wait_recv()
    shares = [copy(quarter, quarter, S_SHARE, R_SHARE, cross) for cross in crosses]
    for share in shares:
        share.start()
    own[1].wait_recv()
    fwd[1].start()
    swap(zs).start()

    wait_received(R_SHARE, 3 * HALF)
    turned.wait_send()
    ogt[rows_of(zo, 2 * OWN), :] = ogt_pair[...]
    for n in range(4):
        at = slice(n * 256, (n + 1) * 256)
        p_snd[3 * OWN:, at] = product(zo, other, n).astype(jnp.bfloat16)
    for n in range(4):
        at = slice(n * 256, (n + 1) * 256)
        p_own[3 * OWN:, at] = product(zo, core, n)
    last = to_peer(3, R_P3)
    last.start()
    for k in range(ROWS // 128):
        at = slice(k * 128, (k + 1) * 128)
        og[:, at] = jnp.transpose(ogt[at, :])
    last.wait_recv()
    chip_sum(3)

    one[0].start()
    wait_received(R_ASIDE, OWN)
    swap(zo).start()
    wait_received(R_FWD, OWN)
    swap(zf).start()
    wait_received(R_SWAP, 4 * OWN)

    def g_half(j, h):
        return g.at[rows_of(j * 2 + h, SUB)]

    far_p = copy(g_half(yf, hp), y_far.at[0], S_Y, R_FP, way_p)
    far_m = copy(g_half(yf, zl), y_far.at[1], S_Y, R_FM, way_m)
    own_p = copy(g_half(ym, hp), y_own.at[0], S_Y, R_PP, way_m)
    own_m = copy(g_half(yp, zl), y_own.at[1], S_Y, R_MM, way_p)
    sum_p = copy(y_snd.at[0], y_sum.at[0], S_Y, R_PP, way_p)
    sum_m = copy(y_snd.at[1], y_sum.at[1], S_Y, R_MM, way_m)

    def block(t, n):
        return jnp.dot(
            og[rows_of(t, 2 * SUB), :], q[:, n * 256:(n + 1) * 256],
            preferred_element_type=jnp.float32,
        )

    @pl.loop(0, 3)
    def _(k):
        t = jnp.where(k == 0, yf, jnp.where(k == 1, ym, yp))
        for n in range(4):
            g[rows_of(t, 2 * SUB), n * 256:(n + 1) * 256] = block(t, n).astype(jnp.bfloat16)

        @pl.when(k == 0)
        def _():
            far_p.start()
            far_m.start()

        @pl.when(k == 1)
        def _():
            own_p.start()

    for n in range(4):
        gown[:, n * 256:(n + 1) * 256] = block(y, n)

    def middle(h):
        far[h].wait_recv()
        rs_snd[h] = (
            p_own[OWN + h * HALF:OWN + (h + 1) * HALF, :] + rs_far[h].astype(jnp.float32)
        ).astype(jnp.bfloat16)
        whole[h].start()

    middle(0)
    far_p.wait_recv()
    y_snd[0] = (
        g[rows_of(yp * 2 + hp, SUB), :].astype(jnp.float32) + y_far[0].astype(jnp.float32)
    ).astype(jnp.bfloat16)
    sum_p.start()
    own_m.start()

    far_m.wait_recv()
    y_snd[1] = (
        g[rows_of(ym * 2 + zl, SUB), :].astype(jnp.float32) + y_far[1].astype(jnp.float32)
    ).astype(jnp.bfloat16)
    sum_m.start()
    middle(1)
    one[1].start()
    one[2].start()

    wait_received(R_PP, 2 * SUB)
    z_snd[...] = (
        gown[rows_of(hp, SUB), :] + y_own[0].astype(jnp.float32) + y_sum[0].astype(jnp.float32)
    ).astype(jnp.bfloat16)
    across = copy(z_snd, z_rcv, S_Y, R_Z, pair)
    across.start()
    wait_received(R_MM, 2 * SUB)
    mine[...] = (
        gown[rows_of(zl, SUB), :] + y_own[1].astype(jnp.float32) + y_sum[1].astype(jnp.float32)
    )

    def finish(n):
        i, j = CHUNKS[n]
        one[n].wait_recv()
        part = jnp.zeros((j - i, 128), jnp.float32)
        for k in range(COLS // 128):
            at = slice(k * 128, (k + 1) * 128)
            summed = (
                p_own[2 * OWN + i:2 * OWN + j, at]
                + rs_one[i:j, at].astype(jnp.float32) + rs_sum[i:j, at].astype(jnp.float32)
            )
            wg_out[i:j, at] = summed * ins[i:j, at]
            part = part + summed * fac[i:j, at]
        parts[i:j, :] = part

    def row_sums(h):
        at = slice(h * 128, (h + 1) * 128)
        x_snd[:, at] = jnp.broadcast_to(
            jnp.sum(jnp.transpose(parts[at, :]), axis=0, keepdims=True) * GRAD_FACTOR, (8, 128)
        )

    parts[OWN:, :] = jnp.zeros((256 - OWN, 128), jnp.float32)
    whole[0].wait_recv()
    finish(0)
    whole[1].wait_recv()
    finish(1)
    row_sums(0)
    finish(2)
    row_sums(1)
    sends = [copy(x_snd, x_rcv.at[k], S_X, R_X, crosses[k]) for k in range(3)]
    for send in sends:
        send.start()

    across.wait_recv()
    ig_out[...] = (mine[...] + z_rcv[...].astype(jnp.float32)).astype(jnp.bfloat16)

    wait_sent(S_MAIN, ROWS)
    wait_sent(S_P, 6 * OWN)
    wait_sent(S_Y, 7 * SUB)
    wait_sent(S_SHARE, 3 * HALF)

    both = copy(x_rcv, x_rcv, S_X, R_X, peer)
    both.wait_recv()
    total = x_snd[...] + x_rcv[0] + x_rcv[1] + x_rcv[2]
    sg_out[...] = total[0:1, 0:OWN]
    both.wait_send()


def store(ig_ref, wg_ref, sg_ref, ig_hbm, wg_hbm, sg_hbm, sems):
    moves = [
        pltpu.make_async_copy(wg_ref.at[i:i + 56], wg_hbm.at[i:i + 56], sems.at[i // 56])
        for i in range(0, OWN, 56)
    ] + [
        pltpu.make_async_copy(ig_ref, ig_hbm, sems.at[4]),
        pltpu.make_async_copy(sg_ref, sg_hbm, sems.at[5]),
    ]
    for move in moves:
        move.start()
    for move in moves:
        move.wait()


def shards(activations, out_grad, weight, step_size):
    bf16, f32 = jnp.bfloat16, jnp.float32
    hbm = pl.BlockSpec(memory_space=pltpu.HBM)
    vmem = pl.BlockSpec(memory_space=pltpu.VMEM)
    input_grad, weight_grad, step_rows = pl.pallas_call(
        kernel,
        out_shape=(
            pltpu.VMEM((SUB, COLS), bf16),
            pltpu.VMEM((OWN, COLS), f32),
            pltpu.VMEM((1, OWN), f32),
        ),
        in_specs=[hbm] * 4,
        out_specs=(vmem, vmem, vmem),
        scratch_shapes=[
            pltpu.VMEM((TOKENS, COLS), bf16),
            pltpu.VMEM((TOKENS, ROWS), bf16),
            pltpu.VMEM((OWN, COLS), f32),
            pltpu.VMEM((1, ROWS), f32),
            pltpu.VMEM((3 * 128, 128), f32),
            pltpu.VMEM((ROWS, TOKENS), bf16),
            pltpu.VMEM((2 * OWN, TOKENS), bf16),
            pltpu.VMEM((ROWS, COLS), bf16),
            pltpu.VMEM((OWN, COLS), f32),
            pltpu.VMEM((OWN, COLS), f32),
            pltpu.VMEM((4 * OWN, COLS), f32),
            pltpu.VMEM((4 * OWN, COLS), bf16),
            pltpu.VMEM((4 * OWN, COLS), bf16),
            pltpu.VMEM((4 * OWN, COLS), bf16),
            pltpu.VMEM((2, HALF, COLS), bf16),
            pltpu.VMEM((OWN, COLS), bf16),
            pltpu.VMEM((OWN, COLS), bf16),
            pltpu.VMEM((2, HALF, COLS), bf16),
            pltpu.VMEM((256, 128), f32),
            pltpu.VMEM((TOKENS, COLS), bf16),
            pltpu.VMEM((2 * SUB, COLS), f32),
            pltpu.VMEM((2, SUB, COLS), bf16),
            pltpu.VMEM((2, SUB, COLS), bf16),
            pltpu.VMEM((2, SUB, COLS), bf16),
            pltpu.VMEM((2, SUB, COLS), bf16),
            pltpu.VMEM((SUB, COLS), f32),
            pltpu.VMEM((SUB, COLS), bf16),
            pltpu.VMEM((SUB, COLS), bf16),
            pltpu.VMEM((8, 256), f32),
            pltpu.VMEM((3, 8, 256), f32),
            pltpu.SemaphoreType.DMA((N_SEND,)),
            pltpu.SemaphoreType.DMA((N_RECV,)),
            pltpu.SemaphoreType.DMA((5,)),
        ],
        compiler_params=pltpu.CompilerParams(
            collective_id=0, has_side_effects=True, vmem_limit_bytes=60*1024*1024
        ),
        name="backward",
    )(activations, out_grad, weight[0], step_size)
    outs = pl.pallas_call(
        store,
        out_shape=(
            jax.ShapeDtypeStruct((SUB, COLS), bf16),
            jax.ShapeDtypeStruct((OWN, COLS), f32),
            jax.ShapeDtypeStruct((1, OWN), f32),
        ),
        in_specs=[vmem] * 3,
        out_specs=(hbm,) * 3,
        scratch_shapes=[pltpu.SemaphoreType.DMA((6,))],
        compiler_params=pltpu.CompilerParams(vmem_limit_bytes=4 * 1024 * 1024),
        name="store",
    )(input_grad, weight_grad, step_rows)
    return (outs[0], outs[1][None], outs[2])


def solution(mesh):
    split = Mesh(mesh.devices.reshape(4, 2, 4, 2, 4), ("zh", "core", "y", "zl", "x"))
    in_specs = (P(DP, "x"), P(DP, ROW), P(ROW, DP, "x"), P(ROW, None))
    out_specs = (P(DP + ROW, "x"), P(ROW, DP, "x"), P(ROW, DP))
    return jax.shard_map(
        shards, mesh=split, in_specs=in_specs, out_specs=out_specs, check_vma=False
    )
```

time: 75.6 us -> 75.1 us (level)
  no operation moved by 1% of the time
where the time goes in v5:
time: 75.1 us; the launch traced here: 73.9 us
  Pallas kernels  73.2 us (97%)
    pallas_call x1, Pallas kernels, shards(): pl.pallas_call(kernel, out_shape=(pltpu.VMEM((SUB, COLS), bf16), pltpu.VM...  72.2 us

profile of v5, /device:TPU:8, one launch (start us, length us, event | category | flops | bytes accessed | tf_op | source)
XLA Modules:
  0.0 73.9 jit_solution(12923960960665985856)
XLA Ops:
  0.6 72.2 %backward.1 = (bf16[128,1024]{1,0:T(8,128)(2,1)S(1)}, f32[224,1024]{1,0:T(8,128)S(1)}, f32[1,224]{1,0:T(1,128)S(1)}) custom-call(bf16[1024,1024]{1,0:T(8,128)(2,1)} %act_hbm.1, bf16[1024,1792]{1,0:T(8,128)(2,1)} %og_hbm.1, f32[224,1024]{1,0:T(8,128)} %bitcast.2, f32[1,1792]{1,0:T(1,128)} %s_hbm.1), custom_call_target="tpu_custom_call" | custom-call | tf_op jit(solution)/shard_map/backward/pallas_call | solution.py:371
  72.8 1.1 %store.1 = (bf16[128,1024]{1,0:T(8,128)(2,1)}, f32[224,1024]{1,0:T(8,128)}, f32[1,224]{1,0:T(1,128)}) custom-call(bf16[128,1024]{1,0:T(8,128)(2,1)S(1)} %get-tuple-element.9.ig_ref, f32[224,1024]{1,0:T(8,128)S(1)} %get-tuple-element.10.wg_ref, f32[1,224]{1,0:T(1,128)S(1)} %get-tuple-element.11.sg_ref), custom_call_target="tpu_custom_call" | custom-call | tf_op jit(solution)/shard_map/store/pallas_call | solution.py:420

commit v6 on v5

--- a/solution.py
+++ b/solution.py
@@ -40,7 +40,7 @@
     rs_far, rs_one, rs_sum, rs_snd, parts,
     g, gown, y_far, y_own, y_sum, y_snd, mine, z_snd, z_rcv,
     x_snd, x_rcv,
-    ss, rs, ls,
+    ss, rs, ls, told,
 ):
     zh = lax.axis_index("zh")
     core = lax.axis_index("core")
@@ -70,9 +70,28 @@
         pltpu.make_async_copy(act_hbm, act, ls.at[4]),
     ]
     barrier = pltpu.get_barrier_semaphore()
-    partners = [chain, back, beside, peer, way_p, way_m, pair] + crosses
-    for partner in partners:
-        pl.semaphore_signal(barrier, inc=1, device_id=partner, device_id_type=MESH)
+    along_z = [chain, back, beside, pair]
+    across_z = [way_p, way_m] + crosses
+    for partner in along_z:
+        pl.semaphore_signal(barrier, inc=1, device_id={**partner, "core": 1}, device_id_type=MESH)
+
+    @pl.when(core == 0)
+    def _():
+        pl.semaphore_signal(barrier, inc=1, device_id=peer, device_id_type=MESH)
+
+    for partner in across_z:
+        pl.semaphore_signal(barrier, inc=1, device_id={**partner, "core": 0}, device_id_type=MESH)
+
+    def meet(listener, signals):
+        @pl.when(core == listener)
+        def _():
+            pl.semaphore_wait(barrier, signals)
+            pl.semaphore_signal(told, inc=1, device_id=peer, device_id_type=MESH)
+
+        @pl.when(core != listener)
+        def _():
+            pl.semaphore_wait(told, 1)
+
     for load in loads[:3]:
         load.start()
 
@@ -112,7 +131,7 @@
 
     loads[1].wait()
     quantize(0)
-    pl.semaphore_wait(barrier, len(partners))
+    meet(1, 2 * len(along_z) + 1)
 
     own = [copy(half(zh, h), half(zh, h), S_MAIN, R_OWN + h, back) for h in range(2)]
     fwd = [copy(half(zs, h), half(zs, h), S_MAIN, R_FWD, back) for h in range(2)]
@@ -204,6 +223,7 @@
 
     turned.wait_recv()
     shares = [copy(quarter, quarter, S_SHARE, R_SHARE, cross) for cross in crosses]
+    meet(0, 2 * len(across_z))
     for share in shares:
         share.start()
     own[1].wait_recv()
@@ -411,6 +431,7 @@
             pltpu.SemaphoreType.DMA((N_SEND,)),
             pltpu.SemaphoreType.DMA((N_RECV,)),
             pltpu.SemaphoreType.DMA((5,)),
+            pltpu.SemaphoreType.REGULAR,
         ],
         compiler_params=pltpu.CompilerParams(
             collective_id=0, has_side_effects=True, vmem_limit_bytes=60*1024*1024

time: 75.1 us -> 74.4 us (level); the launches traced: 73.9 us -> 74.3 us
  no operation moved by 1% of the time
where the time goes in v6:
time: 74.4 us; the launch traced here: 74.3 us
  Pallas kernels  73.6 us (99%)
    pallas_call x1, Pallas kernels, shards(): pl.pallas_call(kernel, out_shape=(pltpu.VMEM((SUB, COLS), bf16), pltpu.VM...  72.6 us

profile of v6, /device:TPU:8, one launch (start us, length us, event | category | flops | bytes accessed | tf_op | source)
XLA Modules:
  0.0 74.3 jit_solution(16163973821193899189)
XLA Ops:
  0.6 72.6 %backward.1 = (bf16[128,1024]{1,0:T(8,128)(2,1)S(1)}, f32[224,1024]{1,0:T(8,128)S(1)}, f32[1,224]{1,0:T(1,128)S(1)}) custom-call(bf16[1024,1024]{1,0:T(8,128)(2,1)} %act_hbm.1, bf16[1024,1792]{1,0:T(8,128)(2,1)} %og_hbm.1, f32[224,1024]{1,0:T(8,128)} %bitcast.2, f32[1,1792]{1,0:T(1,128)} %s_hbm.1), custom_call_target="tpu_custom_call" | custom-call | tf_op jit(solution)/shard_map/backward/pallas_call | solution.py:391
  73.2 1.1 %store.1 = (bf16[128,1024]{1,0:T(8,128)(2,1)}, f32[224,1024]{1,0:T(8,128)}, f32[1,224]{1,0:T(1,128)}) custom-call(bf16[128,1024]{1,0:T(8,128)(2,1)S(1)} %get-tuple-element.9.ig_ref, f32[224,1024]{1,0:T(8,128)S(1)} %get-tuple-element.10.wg_ref, f32[1,224]{1,0:T(1,128)S(1)} %get-tuple-element.11.sg_ref), custom_call_target="tpu_custom_call" | custom-call | tf_op jit(solution)/shard_map/store/pallas_call | solution.py:441

commit v7 on v5

--- a/solution.py
+++ b/solution.py
@@ -40,7 +40,7 @@
     rs_far, rs_one, rs_sum, rs_snd, parts,
     g, gown, y_far, y_own, y_sum, y_snd, mine, z_snd, z_rcv,
     x_snd, x_rcv,
-    ss, rs, ls,
+    ss, rs, ls, told,
 ):
     zh = lax.axis_index("zh")
     core = lax.axis_index("core")
@@ -70,9 +70,13 @@
         pltpu.make_async_copy(act_hbm, act, ls.at[4]),
     ]
     barrier = pltpu.get_barrier_semaphore()
-    partners = [chain, back, beside, peer, way_p, way_m, pair] + crosses
-    for partner in partners:
+    along_z = [chain, back, beside, pair, peer]
+    across_z = [way_p, way_m] + crosses
+    for partner in along_z:
         pl.semaphore_signal(barrier, inc=1, device_id=partner, device_id_type=MESH)
+    for partner in across_z:
+        pl.semaphore_signal(barrier, inc=1, device_id={**partner, "core": 0}, device_id_type=MESH)
+
     for load in loads[:3]:
         load.start()
 
@@ -112,7 +116,16 @@
 
     loads[1].wait()
     quantize(0)
-    pl.semaphore_wait(barrier, len(partners))
+
+    @pl.when(core == 1)
+    def _():
+        pl.semaphore_wait(barrier, len(along_z))
+
+    @pl.when(core == 0)
+    def _():
+        pl.semaphore_wait(barrier, len(along_z) + 2 * len(across_z))
+        pl.semaphore_signal(told, inc=1, device_id=peer, device_id_type=MESH)
+
 
     own = [copy(half(zh, h), half(zh, h), S_MAIN, R_OWN + h, back) for h in range(2)]
     fwd = [copy(half(zs, h), half(zs, h), S_MAIN, R_FWD, back) for h in range(2)]
@@ -204,6 +217,11 @@
 
     turned.wait_recv()
     shares = [copy(quarter, quarter, S_SHARE, R_SHARE, cross) for cross in crosses]
+
+    @pl.when(core == 1)
+    def _():
+        pl.semaphore_wait(told, 1)
+
     for share in shares:
         share.start()
     own[1].wait_recv()
@@ -411,6 +429,7 @@
             pltpu.SemaphoreType.DMA((N_SEND,)),
             pltpu.SemaphoreType.DMA((N_RECV,)),
             pltpu.SemaphoreType.DMA((5,)),
+            pltpu.SemaphoreType.REGULAR,
         ],
         compiler_params=pltpu.CompilerParams(
             collective_id=0, has_side_effects=True, vmem_limit_bytes=60*1024*1024

time: 75.1 us -> 73.9 us (0.984); the launches traced: 73.9 us -> 73.8 us
  no operation moved by 1% of the time
where the time goes in v7:
time: 73.9 us; the launch traced here: 73.8 us
  Pallas kernels  73.1 us (99%)
    pallas_call x1, Pallas kernels, shards(): pl.pallas_call(kernel, out_shape=(pltpu.VMEM((SUB, COLS), bf16), pltpu.VM...  72.1 us

profile of v7, /device:TPU:8, one launch (start us, length us, event | category | flops | bytes accessed | tf_op | source)
XLA Modules:
  0.0 73.8 jit_solution(8196517389431876188)
XLA Ops:
  0.6 72.1 %backward.1 = (bf16[128,1024]{1,0:T(8,128)(2,1)S(1)}, f32[224,1024]{1,0:T(8,128)S(1)}, f32[1,224]{1,0:T(1,128)S(1)}) custom-call(bf16[1024,1024]{1,0:T(8,128)(2,1)} %act_hbm.1, bf16[1024,1792]{1,0:T(8,128)(2,1)} %og_hbm.1, f32[224,1024]{1,0:T(8,128)} %bitcast.2, f32[1,1792]{1,0:T(1,128)} %s_hbm.1), custom_call_target="tpu_custom_call" | custom-call | tf_op jit(solution)/shard_map/backward/pallas_call | solution.py:389
  72.7 1.1 %store.1 = (bf16[128,1024]{1,0:T(8,128)(2,1)}, f32[224,1024]{1,0:T(8,128)}, f32[1,224]{1,0:T(1,128)}) custom-call(bf16[128,1024]{1,0:T(8,128)(2,1)S(1)} %get-tuple-element.9.ig_ref, f32[224,1024]{1,0:T(8,128)S(1)} %get-tuple-element.10.wg_ref, f32[1,224]{1,0:T(1,128)S(1)} %get-tuple-element.11.sg_ref), custom_call_target="tpu_custom_call" | custom-call | tf_op jit(solution)/shard_map/store/pallas_call | solution.py:439

commit v8 on v7

--- a/solution.py
+++ b/solution.py
@@ -70,15 +70,15 @@
         pltpu.make_async_copy(act_hbm, act, ls.at[4]),
     ]
     barrier = pltpu.get_barrier_semaphore()
-    along_z = [chain, back, beside, pair, peer]
-    across_z = [way_p, way_m] + crosses
-    for partner in along_z:
+    near = [beside, peer]
+    others = [chain, back, pair, way_p, way_m] + crosses
+    for partner in near:
         pl.semaphore_signal(barrier, inc=1, device_id=partner, device_id_type=MESH)
-    for partner in across_z:
+    for partner in others:
         pl.semaphore_signal(barrier, inc=1, device_id={**partner, "core": 0}, device_id_type=MESH)
 
-    for load in loads[:3]:
-        load.start()
+    loads[0].start()
+    loads[1].start()
 
     def copy(src, dst, sender, receiver, device):
         return pltpu.make_async_remote_copy(
@@ -101,6 +101,7 @@
     first_row = (zh * 2 + core) * OWN
     tile = jnp.minimum(first_row // 128, (ROWS - 3 * 128) // 128)
     loads[0].wait()
+    loads[2].start()
     scol[...] = jnp.transpose(
         jnp.broadcast_to(s[:, pl.ds(pl.multiple_of(tile * 128, 128), 3 * 128)], (128, 3 * 128))
     )
@@ -119,13 +120,12 @@
 
     @pl.when(core == 1)
     def _():
-        pl.semaphore_wait(barrier, len(along_z))
+        pl.semaphore_wait(barrier, len(near))
 
     @pl.when(core == 0)
     def _():
-        pl.semaphore_wait(barrier, len(along_z) + 2 * len(across_z))
+        pl.semaphore_wait(barrier, len(near) + 2 * len(others))
         pl.semaphore_signal(told, inc=1, device_id=peer, device_id_type=MESH)
-
 
     own = [copy(half(zh, h), half(zh, h), S_MAIN, R_OWN + h, back) for h in range(2)]
     fwd = [copy(half(zs, h), half(zs, h), S_MAIN, R_FWD, back) for h in range(2)]
@@ -134,12 +134,17 @@
     def swap(j):
         return copy(shard(j), shard(j), S_MAIN, R_SWAP, peer)
 
-    own[0].start()
     aside[0].start()
     loads[3].start()
     loads[4].start()
     loads[2].wait()
     quantize(1)
+
+    @pl.when(core == 1)
+    def _():
+        pl.semaphore_wait(told, 1)
+
+    own[0].start()
 
     loads[3].wait()
     aside[1].start()
@@ -217,11 +222,6 @@
 
     turned.wait_recv()
     shares = [copy(quarter, quarter, S_SHARE, R_SHARE, cross) for cross in crosses]
-
-    @pl.when(core == 1)
-    def _():
-        pl.semaphore_wait(told, 1)
-
     for share in shares:
         share.start()
     own[1].wait_recv()
@@ -337,9 +337,7 @@
 
     def row_sums(h):
         at = slice(h * 128, (h + 1) * 128)
-        x_snd[:, at] = jnp.broadcast_to(
-            jnp.sum(jnp.transpose(parts[at, :]), axis=0, keepdims=True) * GRAD_FACTOR, (8, 128)
-        )
+        x_snd[:, at] = jnp.sum(jnp.transpose(parts[at, :]), axis=0, keepdims=True) * GRAD_FACTOR
 
     parts[OWN:, :] = jnp.zeros((256 - OWN, 128), jnp.float32)
     whole[0].wait_recv()
@@ -364,7 +362,7 @@
     both = copy(x_rcv, x_rcv, S_X, R_X, peer)
     both.wait_recv()
     total = x_snd[...] + x_rcv[0] + x_rcv[1] + x_rcv[2]
-    sg_out[...] = total[0:1, 0:OWN]
+    sg_out[...] = total[:, 0:OWN]
     both.wait_send()
 
 
@@ -424,8 +422,8 @@
             pltpu.VMEM((SUB, COLS), f32),
             pltpu.VMEM((SUB, COLS), bf16),
             pltpu.VMEM((SUB, COLS), bf16),
-            pltpu.VMEM((8, 256), f32),
-            pltpu.VMEM((3, 8, 256), f32),
+            pltpu.VMEM((1, 256), f32),
+            pltpu.VMEM((3, 1, 256), f32),
             pltpu.SemaphoreType.DMA((N_SEND,)),
             pltpu.SemaphoreType.DMA((N_RECV,)),
             pltpu.SemaphoreType.DMA((5,)),

time: 73.9 us -> 73.8 us (level)
  no operation moved by 1% of the time
where the time goes in v8:
time: 73.8 us; the launch traced here: 73.7 us
  Pallas kernels  73 us (99%)
    pallas_call x1, Pallas kernels, shards(): pl.pallas_call(kernel, out_shape=(pltpu.VMEM((SUB, COLS), bf16), pltpu.VM...  72 us

profile of v8, /device:TPU:8, one launch (start us, length us, event | category | flops | bytes accessed | tf_op | source)
XLA Modules:
  0.0 73.7 jit_solution(10208845732364202149)
XLA Ops:
  0.6 72.0 %backward.1 = (bf16[128,1024]{1,0:T(8,128)(2,1)S(1)}, f32[224,1024]{1,0:T(8,128)S(1)}, f32[1,224]{1,0:T(1,128)S(1)}) custom-call(bf16[1024,1024]{1,0:T(8,128)(2,1)} %act_hbm.1, bf16[1024,1792]{1,0:T(8,128)(2,1)} %og_hbm.1, f32[224,1024]{1,0:T(8,128)} %bitcast.2, f32[1,1792]{1,0:T(1,128)} %s_hbm.1), custom_call_target="tpu_custom_call" | custom-call | tf_op jit(solution)/shard_map/backward/pallas_call | solution.py:387
  72.6 1.1 %store.1 = (bf16[128,1024]{1,0:T(8,128)(2,1)}, f32[224,1024]{1,0:T(8,128)}, f32[1,224]{1,0:T(1,128)}) custom-call(bf16[128,1024]{1,0:T(8,128)(2,1)S(1)} %get-tuple-element.9.ig_ref, f32[224,1024]{1,0:T(8,128)S(1)} %get-tuple-element.10.wg_ref, f32[1,224]{1,0:T(1,128)S(1)} %get-tuple-element.11.sg_ref), custom_call_target="tpu_custom_call" | custom-call | tf_op jit(solution)/shard_map/store/pallas_call | solution.py:437

commit v9 on v8

--- a/solution.py
+++ b/solution.py
@@ -66,8 +66,8 @@
         pltpu.make_async_copy(s_hbm, s, ls.at[0]),
         pltpu.make_async_copy(w_hbm.at[0:HALF], w.at[0:HALF], ls.at[1]),
         pltpu.make_async_copy(w_hbm.at[HALF:OWN], w.at[HALF:OWN], ls.at[2]),
-        pltpu.make_async_copy(og_hbm, og, ls.at[3]),
-        pltpu.make_async_copy(act_hbm, act, ls.at[4]),
+        pltpu.make_async_copy(og_hbm, og, ls.at[0]),
+        pltpu.make_async_copy(act_hbm, act, ls.at[1]),
     ]
     barrier = pltpu.get_barrier_semaphore()
     near = [beside, peer]
@@ -368,11 +368,9 @@
 
 def store(ig_ref, wg_ref, sg_ref, ig_hbm, wg_hbm, sg_hbm, sems):
     moves = [
-        pltpu.make_async_copy(wg_ref.at[i:i + 56], wg_hbm.at[i:i + 56], sems.at[i // 56])
-        for i in range(0, OWN, 56)
-    ] + [
-        pltpu.make_async_copy(ig_ref, ig_hbm, sems.at[4]),
-        pltpu.make_async_copy(sg_ref, sg_hbm, sems.at[5]),
+        pltpu.make_async_copy(wg_ref, wg_hbm, sems.at[0]),
+        pltpu.make_async_copy(ig_ref, ig_hbm, sems.at[1]),
+        pltpu.make_async_copy(sg_ref, sg_hbm, sems.at[2]),
     ]
     for move in moves:
         move.start()
@@ -426,7 +424,7 @@
             pltpu.VMEM((3, 1, 256), f32),
             pltpu.SemaphoreType.DMA((N_SEND,)),
             pltpu.SemaphoreType.DMA((N_RECV,)),
-            pltpu.SemaphoreType.DMA((5,)),
+            pltpu.SemaphoreType.DMA((3,)),
             pltpu.SemaphoreType.REGULAR,
         ],
         compiler_params=pltpu.CompilerParams(
@@ -443,7 +441,7 @@
         ),
         in_specs=[vmem] * 3,
         out_specs=(hbm,) * 3,
-        scratch_shapes=[pltpu.SemaphoreType.DMA((6,))],
+        scratch_shapes=[pltpu.SemaphoreType.DMA((3,))],
         compiler_params=pltpu.CompilerParams(vmem_limit_bytes=4 * 1024 * 1024),
         name="store",
     )(input_grad, weight_grad, step_rows)

time: 73.8 us -> 73.8 us (level)
  no operation moved by 1% of the time
where the time goes in v9:
time: 73.8 us; the launch traced here: 73.6 us
  Pallas kernels  73 us (99%)
    pallas_call x1, Pallas kernels, shards(): pl.pallas_call(kernel, out_shape=(pltpu.VMEM((SUB, COLS), bf16), pltpu.VM...  72 us

profile of v9, /device:TPU:8, one launch (start us, length us, event | category | flops | bytes accessed | tf_op | source)
XLA Modules:
  0.0 73.6 jit_solution(13768622978991331367)
XLA Ops:
  0.6 72.0 %backward.1 = (bf16[128,1024]{1,0:T(8,128)(2,1)S(1)}, f32[224,1024]{1,0:T(8,128)S(1)}, f32[1,224]{1,0:T(1,128)S(1)}) custom-call(bf16[1024,1024]{1,0:T(8,128)(2,1)} %act_hbm.1, bf16[1024,1792]{1,0:T(8,128)(2,1)} %og_hbm.1, f32[224,1024]{1,0:T(8,128)} %bitcast.2, f32[1,1792]{1,0:T(1,128)} %s_hbm.1), custom_call_target="tpu_custom_call" | custom-call | tf_op jit(solution)/shard_map/backward/pallas_call | solution.py:385
  72.6 1.0 %store.1 = (bf16[128,1024]{1,0:T(8,128)(2,1)}, f32[224,1024]{1,0:T(8,128)}, f32[1,224]{1,0:T(1,128)}) custom-call(bf16[128,1024]{1,0:T(8,128)(2,1)S(1)} %get-tuple-element.9.ig_ref, f32[224,1024]{1,0:T(8,128)S(1)} %get-tuple-element.10.wg_ref, f32[1,224]{1,0:T(1,128)S(1)} %get-tuple-element.11.sg_ref), custom_call_target="tpu_custom_call" | custom-call | tf_op jit(solution)/shard_map/store/pallas_call | solution.py:435
